TPU v7x, 256 devices: a whole 4x4x8 slice. The times are simulated.
256 devices in a mesh: emb: 8 (over z), col: 4 (over y), row: 8 (over x, core).
Axes of the slice: x: 4, y: 4, z: 8, core: 2. Of those that a mesh axis runs over, the one named last changes fastest.
Arguments:
- inter_mask: int32 [2048, 65536], P('row', 'col')
- emb_user: bfloat16 [2048, 128], P(('row', 'col'), 'emb')
- emb_item: bfloat16 [65536, 128], P(('col', 'row'), 'emb')
- triples: int32 [4096, 3], replicated
Outputs:
- output 1: bfloat16 [2048, 128], P(('row', 'col'), 'emb')
- output 2: bfloat16 [65536, 128], P(('col', 'row'), 'emb')
- output 3: float32 [4096], replicated
All inputs are finite; a program needn't handle non-finite values.
Results may differ from a plain program's by a relative error of at most 0.0126005.
Values are sent between devices in bfloat16 or wider.
A program may use at most 768 MiB of HBM per device.

v0:
```python
import jax
import jax.numpy as jnp
from jax import lax
from jax.sharding import PartitionSpec as P

NUM_LAYERS = 3


def lookup_rows(table, ids, offset):
    own_rows = table.shape[0]
    local_ids = ids - offset
    owned = (local_ids >= 0) & (local_ids < own_rows)
    picked = jnp.take(table, jnp.clip(local_ids, 0, own_rows - 1), axis=0)
    return jnp.where(owned[:, None], picked.astype(jnp.float32), 0.0)


def bpr_terms(final_user, final_item, triples, user_off, item_off):
    num_trip = triples.shape[0]
    fetched = jnp.concatenate([
        lookup_rows(final_user, triples[:, 0], user_off),
        lookup_rows(final_item, triples[:, 1], item_off),
        lookup_rows(final_item, triples[:, 2], item_off)], axis=0)
    fetched = lax.psum(fetched, ("row", "col"))
    e_user = fetched[:num_trip]
    e_pos = fetched[num_trip:2 * num_trip]
    e_neg = fetched[2 * num_trip:]
    score = lax.psum(jnp.sum(e_user * (e_pos - e_neg), axis=1), "emb")
    return jax.nn.softplus(-score)


def norm_adjacency(mask_blk):
    deg_user = lax.psum(jnp.sum(mask_blk, axis=1), "col")
    deg_item = lax.psum(jnp.sum(mask_blk, axis=0), "row")
    inv_user = lax.rsqrt(jnp.maximum(deg_user, 1).astype(jnp.float32))
    inv_item = lax.rsqrt(jnp.maximum(deg_item, 1).astype(jnp.float32))
    return ((inv_user[:, None] * mask_blk.astype(jnp.float32)) * inv_item[None, :]).astype(jnp.bfloat16)


def solution(mesh):
    n_col = mesh.shape["col"]
    n_row = mesh.shape["row"]

    def local_fn(mask_blk, user_sh, item_sh, triples):
        adj_blk = norm_adjacency(mask_blk)
        user_cur = user_sh
        item_cur = item_sh
        user_acc = user_sh.astype(jnp.float32)
        item_acc = item_sh.astype(jnp.float32)
        for layer_idx in range(NUM_LAYERS):
            item_panel = lax.all_gather(item_cur, "row", axis=0, tiled=True)
            user_part = jnp.dot(adj_blk, item_panel, preferred_element_type=jnp.float32)
            user_next = lax.psum_scatter(user_part, "col", scatter_dimension=0, tiled=True).astype(jnp.bfloat16)
            user_panel = lax.all_gather(user_cur, "col", axis=0, tiled=True)
            item_part = lax.dot_general(adj_blk, user_panel, (((0,), (0,)), ((), ())), preferred_element_type=jnp.float32)
            item_next = lax.psum_scatter(item_part, "row", scatter_dimension=0, tiled=True).astype(jnp.bfloat16)
            user_acc = user_acc + user_next.astype(jnp.float32)
            item_acc = item_acc + item_next.astype(jnp.float32)
            user_cur = user_next
            item_cur = item_next
        final_user = (user_acc / (NUM_LAYERS + 1)).astype(jnp.bfloat16)
        final_item = (item_acc / (NUM_LAYERS + 1)).astype(jnp.bfloat16)
        user_off = (lax.axis_index("row") * n_col + lax.axis_index("col")) * final_user.shape[0]
        item_off = (lax.axis_index("col") * n_row + lax.axis_index("row")) * final_item.shape[0]
        return final_user, final_item, bpr_terms(final_user, final_item, triples, user_off, item_off)

    return jax.shard_map(
        local_fn, mesh=mesh,
        in_specs=(P("row", "col"), P(("row", "col"), "emb"), P(("col", "row"), "emb"), P()),
        out_specs=(P(("row", "col"), "emb"), P(("col", "row"), "emb"), P()),
        check_vma=False)
```

profile of v0, /device:TPU:1, one launch (start us, length us, event | category | flops | bytes accessed | tf_op | source)
XLA Modules:
  0.0 497.4 jit_solution(3400130672541699677)
XLA Ops:
  7.2 0.0 all-reduce.3.cloned.1.call-start
  7.2 9.2 %fusion.4 = (s32[256]{0:T(256)S(1)}, s32[16384]{0:T(1024)}) fusion(s32[256,16384]{1,0:T(8,128)} %param.6), kind=kLoop, calls=%fused_computation.35 | loop fusion | flops 8371968 | bytes 16843776 | tf_op jit(solution)/shard_map/reduce_sum | solution.py:32
  16.5 0.0 all-reduce.3.cloned.1.call-update
  16.5 0.0 reduce-scatter.19.cloned.1.call-start
  16.5 7.9 %psum.28 = s32[256]{0:T(256)S(1)} all-reduce(s32[256]{0:T(256)S(1)} %get-tuple-element.7), channel_id=1, replica_groups=mesh['emb'=8,'col'=4,'row'=8] {'col'}, use_global_device_ids=true, to_apply=%region_1.0 | all-reduce | flops 256 | bytes 2048 | tf_op jit(solution)/shard_map/psum | solution.py:32
  24.4 16.0 %all_gather.18 = bf16[16384,16]{0,1:T(8,128)(2,1)S(1)} all-gather(bf16[2048,16]{0,1:T(8,128)(2,1)S(1)} %copy-done.2), channel_id=1, replica_groups=mesh['emb'=8,'col'=4,'row'=8] {'row'}, dimensions={0}, use_global_device_ids=true | all-gather | bytes 589824 | tf_op jit(solution)/shard_map/all_gather | solution.py:50
  40.4 8.9 %all-gather = bf16[4,64,16]{1,2,0:T(8,128)(2,1)S(1)} all-gather(bf16[1,64,16]{1,2,0:T(8,128)(2,1)S(1)} %bitcast.38), channel_id=1, replica_groups=mesh['emb'=8,'col'=4,'row'=8] {'col'}, dimensions={0}, use_global_device_ids=true | all-gather | bytes 10240 | tf_op jit(solution)/shard_map/all_gather | solution.py:53
  49.3 0.1 reshape.54
  49.4 33.7 %all-reduce.3.cloned.1.call-done = s32[16384]{0:T(1024)} async-done(((s32[16384]{0:T(1024)}), s32[16384]{0:T(1024)}) %all-reduce.3.cloned.1.call-update) | async-done | bytes 65552 | tf_op jit(solution)/shard_map/psum | solution.py:33
  83.2 0.9 convert_rsqrt_fusion
  84.0 7.1 %multiply_convert_fusion = bf16[256,16384]{1,0:T(8,128)(2,1)S(1)} fusion(s32[256,16384]{1,0:T(8,128)} %param.6, f32[16384]{0:T(1024)S(1)} %convert_rsqrt_fusion, f32[256]{0:T(256)S(1)} %convert_rsqrt_fusion.1), kind=kLoop, calls=%fused_computation.3 | loop fusion | flops 16777216 | bytes 25232384 | tf_op jit(solution)/shard_map/convert_element_type | solution.py:36
  91.2 3.2 copy-done
  94.4 3.0 fusion.5
  97.3 0.0 reduce-scatter.19.cloned.1.call-update
  97.3 0.0 reduce-scatter.13.cloned.1.call-start
  97.4 5.7 %fusion.8 = f32[16384,16]{0,1:T(8,128)} fusion(bf16[256,16]{0,1:T(8,128)(2,1)S(1)} %reshape.54, bf16[256,16384]{1,0:T(8,128)(2,1)} %copy-done), kind=kOutput, calls=%fused_computation.39 | convolution fusion | flops 134217728 | bytes 9445376 | tf_op jit(solution)/shard_map/dot_general | solution.py:54
  103.1 0.0 reduce-scatter.13.cloned.1.call-update
  103.1 0.0 reduce-scatter.21.cloned.1.call-start
  103.1 16.3 %reduce-scatter.19.cloned.1.call-done = f32[64,16]{1,0:T(8,128)} async-done(((f32[256,16]{1,0:T(8,128)}), f32[64,16]{1,0:T(8,128)}) %reduce-scatter.19.cloned.1.call-update) | async-done | bytes 4112
  119.4 0.8 copy.41
  120.3 8.9 %all-gather.1 = bf16[4,64,16]{1,2,0:T(8,128)(2,1)S(1)} all-gather(bf16[1,64,16]{1,2,0:T(8,128)(2,1)S(1)} %bitcast.36), channel_id=1, replica_groups=mesh['emb'=8,'col'=4,'row'=8] {'col'}, dimensions={0}, use_global_device_ids=true | all-gather | bytes 10240 | tf_op jit(solution)/shard_map/all_gather | solution.py:53
  129.2 0.1 reshape.56
  129.3 27.3 %reduce-scatter.13.cloned.1.call-done = f32[2048,16]{0,1:T(8,128)} async-done(((f32[16384,16]{0,1:T(8,128)}), f32[2048,16]{0,1:T(8,128)}) %reduce-scatter.13.cloned.1.call-update) | async-done | bytes 131088 | tf_op jit(solution)/shard_map/reduce_scatter | solution.py:55
  156.5 0.9 convert_element_type.76
  157.5 15.9 %all_gather.20 = bf16[16384,16]{0,1:T(8,128)(2,1)S(1)} all-gather(bf16[2048,16]{0,1:T(8,128)(2,1)S(1)} %convert_element_type.76), channel_id=1, replica_groups=mesh['emb'=8,'col'=4,'row'=8] {'row'}, dimensions={0}, use_global_device_ids=true | all-gather | bytes 589824 | tf_op jit(solution)/shard_map/all_gather | solution.py:50
  173.3 6.4 %fusion.6 = f32[256,16]{1,0:T(8,128)} fusion(bf16[256,16384]{1,0:T(8,128)(2,1)} %copy-done, bf16[16384,16]{0,1:T(8,128)(2,1)S(1)} %all_gather.20), kind=kOutput, calls=%fused_computation.37 | convolution fusion | flops 134217728 | bytes 8929280
  179.7 0.0 reduce-scatter.21.cloned.1.call-update
  179.7 0.2 reduce-scatter.15.cloned.1.call-start
  180.0 5.7 %fusion.9 = f32[16384,16]{0,1:T(8,128)} fusion(bf16[256,16]{0,1:T(8,128)(2,1)S(1)} %reshape.56, bf16[256,16384]{1,0:T(8,128)(2,1)} %copy-done), kind=kOutput, calls=%fused_computation.40 | convolution fusion | flops 134217728 | bytes 9445376 | tf_op jit(solution)/shard_map/dot_general | solution.py:54
  185.6 0.0 reduce-scatter.15.cloned.1.call-update
  185.6 0.0 reduce-scatter.17.cloned.1.call-start
  185.7 14.2 %reduce-scatter.21.cloned.1.call-done = f32[64,16]{1,0:T(8,128)} async-done(((f32[256,16]{1,0:T(8,128)}), f32[64,16]{1,0:T(8,128)}) %reduce-scatter.21.cloned.1.call-update) | async-done | bytes 4112
  199.9 0.8 copy.43
  200.8 8.9 %all-gather.2 = bf16[4,64,16]{1,2,0:T(8,128)(2,1)S(1)} all-gather(bf16[1,64,16]{1,2,0:T(8,128)(2,1)S(1)} %bitcast.37), channel_id=1, replica_groups=mesh['emb'=8,'col'=4,'row'=8] {'col'}, dimensions={0}, use_global_device_ids=true | all-gather | bytes 10240 | tf_op jit(solution)/shard_map/all_gather | solution.py:53
  209.7 0.1 reshape.58
  209.8 5.6 %fusion.10 = f32[16384,16]{0,1:T(8,128)} fusion(bf16[256,16]{0,1:T(8,128)(2,1)S(1)} %reshape.58, bf16[256,16384]{1,0:T(8,128)(2,1)} %copy-done), kind=kOutput, calls=%fused_computation.41 | convolution fusion | flops 134217728 | bytes 9445376 | tf_op jit(solution)/shard_map/dot_general | solution.py:54
  215.4 0.0 reduce-scatter.17.cloned.1.call-update
  215.4 0.0 reduce-scatter.23.cloned.1.call-start
  215.4 0.1 broadcast_clamp_fusion.2
  215.6 0.3 and_reduce_fusion.2
  215.9 21.0 %reduce-scatter.15.cloned.1.call-done = f32[2048,16]{0,1:T(8,128)} async-done(((f32[16384,16]{0,1:T(8,128)}), f32[2048,16]{0,1:T(8,128)}) %reduce-scatter.15.cloned.1.call-update) | async-done | bytes 131088 | tf_op jit(solution)/shard_map/reduce_scatter | solution.py:55
  236.9 36.1 %reduce-scatter.17.cloned.1.call-done = f32[2048,16]{0,1:T(8,128)} async-done(((f32[16384,16]{0,1:T(8,128)}), f32[2048,16]{0,1:T(8,128)}) %reduce-scatter.17.cloned.1.call-update) | async-done | bytes 131088 | tf_op jit(solution)/shard_map/reduce_scatter | solution.py:55
  273.0 1.0 multiply_convert_fusion.1
  274.0 15.9 %all_gather.22 = bf16[16384,16]{0,1:T(8,128)(2,1)S(1)} all-gather(bf16[2048,16]{0,1:T(8,128)(2,1)S(1)} %get-tuple-element.15), channel_id=1, replica_groups=mesh['emb'=8,'col'=4,'row'=8] {'row'}, dimensions={0}, use_global_device_ids=true | all-gather | bytes 589824 | tf_op jit(solution)/shard_map/all_gather | solution.py:50
  289.9 6.4 %fusion.7 = f32[256,16]{1,0:T(8,128)} fusion(bf16[256,16384]{1,0:T(8,128)(2,1)} %copy-done, bf16[16384,16]{0,1:T(8,128)(2,1)S(1)} %all_gather.22), kind=kOutput, calls=%fused_computation.38 | convolution fusion | flops 134217728 | bytes 8929280
  296.3 0.0 reduce-scatter.23.cloned.1.call-update
  296.3 0.0 all-reduce.5.cloned.1.call-start
  296.4 0.3 copy.35
  296.7 12.1 %gather_fusion.2 = bf16[4096,16]{1,0:T(8,128)(2,1)S(1)} fusion(bf16[2048,16]{1,0:T(8,128)(2,1)S(1)} %copy.35, s32[4096]{0:T(1024)S(1)} %fusion.3), kind=kCustom, calls=%fused_computation.1.clone | custom fusion | bytes 278528 | tf_op jit(solution)/shard_map/jit(_take)/gather | solution.py:13
  308.8 14.9 %gather_fusion.1 = bf16[4096,16]{1,0:T(8,128)(2,1)} fusion(bf16[2048,16]{1,0:T(8,128)(2,1)S(1)} %copy.35, s32[4096]{0:T(1024)S(1)} %fusion.2), kind=kCustom, calls=%fused_computation.clone | custom fusion | bytes 278528 | tf_op jit(solution)/shard_map/jit(_take)/gather | solution.py:13
  323.7 7.0 %convert_select_fusion = (f32[4096,16]{1,0:T(8,128)}, f32[4096,16]{1,0:T(8,128)S(1)}) fusion(bf16[4096,16]{1,0:T(8,128)(2,1)S(1)} %gather_fusion.2, pred[4096]{0:T(1024)(128)(4,1)S(1)} %compare_and_fusion, pred[4096]{0:T(1024)(128)(4,1)S(1)} %get-tuple-element.17, bf16[4096,16]{1,0:T(8,128)(2,1)} %gather_fusion.1, pred[4096]{0:T(1024)(128)(4,1)S(1)} %compare_and_fusion.1, ...), kind=kLoop, calls=%fused_computation.4 | loop fusion | flops 393216 | bytes 802816 | tf_op jit(solution)/shard_map/jit(_where)/select_n | solution.py:14
  330.7 2.2 copy.39
  332.9 1.3 copy.38
  334.2 0.8 copy.45
  335.0 0.1 copy.34
  335.1 12.1 %gather_fusion = bf16[4096,16]{1,0:T(8,128)(2,1)S(1)} fusion(bf16[64,16]{1,0:T(8,128)(2,1)S(1)} %copy.34, s32[4096]{0:T(1024)S(1)} %broadcast_clamp_fusion), kind=kCustom, calls=%fused_computation.2 | custom fusion | bytes 278528 | tf_op jit(solution)/shard_map/jit(_take)/gather | solution.py:13
  347.3 1.3 convert_select_fusion.2
  348.5 0.6 copy.37
  349.1 1.9 pad_maximum_fusion
  351.0 0.0 all-reduce.5.cloned.1.call-update
  351.0 114.4 %all-reduce.5.cloned.1.call-done = f32[12288,16]{0,1:T(8,128)} async-done(((f32[12288,16]{0,1:T(8,128)}), f32[12288,16]{0,1:T(8,128)}) %all-reduce.5.cloned.1.call-update) | async-done | bytes 786448 | tf_op jit(solution)/shard_map/psum | solution.py:23
  465.5 1.2 fusion.1
  466.6 23.3 %psum.31 = f32[4096]{0:T(1024)S(1)} all-reduce(f32[4096]{0:T(1024)S(1)} %fusion.1), channel_id=1, replica_groups=mesh['emb'=8,'col'=4,'row'=8] {'emb'}, use_global_device_ids=true, to_apply=%region_12.14 | all-reduce | flops 4096 | bytes 32768 | tf_op jit(solution)/shard_map/psum | solution.py:27
  489.9 0.6 compare_select_fusion.3
  (24 shorter events, 0.1 us)
Async XLA Ops:
  7.2 17.3 %copy-start.2 = (bf16[2048,16]{0,1:T(8,128)(2,1)S(1)}, bf16[2048,16]{0,1:T(8,128)(2,1)}, u32[]{:S(2)}) copy-start(bf16[2048,16]{0,1:T(8,128)(2,1)} %param.8) | copy-start | bytes 196612
  7.2 33.2 %copy-start.5 = (bf16[64,16]{0,1:T(8,128)(2,1)S(1)}, bf16[64,16]{0,1:T(8,128)(2,1)}, u32[]{:S(2)}) copy-start(bf16[64,16]{0,1:T(8,128)(2,1)} %param.7) | copy-start | bytes 6148
  7.2 76.0 %all-reduce.3.cloned.1.call-start = ((), (), s32[]{:S(2)}) async-start(), calls=%async_computation.6 | async-start | bytes 131072 | tf_op jit(solution)/shard_map/psum | solution.py:33
  16.5 102.9 %reduce-scatter.19.cloned.1.call-start = ((), (), s32[]{:S(2)}) async-start(), calls=%async_computation.11 | async-start | bytes 163840
  91.1 3.2 copy-start
  97.3 59.2 %reduce-scatter.13.cloned.1.call-start = ((), (), s32[]{:S(2)}) async-start(), calls=%async_computation.7 | async-start | bytes 1179648 | tf_op jit(solution)/shard_map/reduce_scatter | solution.py:55
  103.1 96.9 %reduce-scatter.21.cloned.1.call-start = ((), (), s32[]{:S(2)}) async-start(), calls=%async_computation.12 | async-start | bytes 163840
  179.7 35.7 %copy-start.4 = (s32[4096,3]{0,1:T(4,128)S(1)}, s32[4096,3]{0,1:T(4,128)}, u32[]{:S(2)}) copy-start(s32[4096,3]{0,1:T(4,128)} %param.9) | copy-start | bytes 147460
  179.7 93.3 %copy-start.1 = (f32[2048,16]{0,1:T(8,128)S(1)}, f32[2048,16]{0,1:T(8,128)}, u32[]{:S(2)}) copy-start(f32[2048,16]{0,1:T(8,128)} %reduce-scatter.13.cloned.1.call-done) | copy-start | bytes 393220
  179.7 57.2 %reduce-scatter.15.cloned.1.call-start = ((), (), s32[]{:S(2)}) async-start(), calls=%async_computation.8 | async-start | bytes 1179648 | tf_op jit(solution)/shard_map/reduce_scatter | solution.py:55
  185.6 87.4 %reduce-scatter.17.cloned.1.call-start = ((), (), s32[]{:S(2)}) async-start(), calls=%async_computation.9 | async-start | bytes 1179648 | tf_op jit(solution)/shard_map/reduce_scatter | solution.py:55
  215.4 118.8 %reduce-scatter.23.cloned.1.call-start = ((), (), s32[]{:S(2)}) async-start(), calls=%async_computation.13 | async-start | bytes 163840
  274.0 34.8 %copy-start.3 = (bf16[2048,16]{0,1:T(8,128)(2,1)}, bf16[2048,16]{0,1:T(8,128)(2,1)S(1)}, u32[]{:S(2)}) copy-start(bf16[2048,16]{0,1:T(8,128)(2,1)S(1)} %get-tuple-element.14) | copy-start | bytes 196612
  296.3 169.1 %all-reduce.5.cloned.1.call-start = ((), (), s32[]{:S(2)}) async-start(), calls=%async_computation.10 | async-start | bytes 1572864 | tf_op jit(solution)/shard_map/psum | solution.py:23
  335.0 16.0 %copy-start.6 = (bf16[64,16]{0,1:T(8,128)(2,1)}, bf16[64,16]{0,1:T(8,128)(2,1)S(1)}, u32[]{:S(2)}) copy-start(bf16[64,16]{0,1:T(8,128)(2,1)S(1)} %multiply_convert_fusion.2) | copy-start | bytes 6148
Sparse Core Ops, SparseCore 0:
  16.6 66.5 all-reduce.2
  97.5 21.9 reduce-scatter.18
  122.0 34.5 reduce-scatter.12
  179.8 20.0 reduce-scatter.20
  202.3 34.5 reduce-scatter.14
  239.3 33.6 reduce-scatter.16
  296.5 20.1 reduce-scatter.22
  351.1 114.2 all-reduce.4
where the time goes:
time: 505 us; the launch traced here: 497 us
  waiting for transfers between devices  263 us (52%)
  blocking collectives  106 us (21%)
  local copies, waits for them, and re-layouts  49.6 us (10%)
  matrix products  32.6 us (6%)
  other arithmetic  31.4 us (6%)
  between operations  14.4 us (3%)
    psum x1, waiting for transfers between devices, bpr_terms(): fetched = lax.psum(fetched, ('row', 'col'))  114 us
    reduce_scatter x3, waiting for transfers between devices, local_fn(): lax.psum_scatter(item_part, 'row', scatter_dimension=0, tiled=True)  84.4 us
    all_gather x3, blocking collectives, local_fn(): item_panel = lax.all_gather(item_cur, 'row', axis=0, tiled=True)  47.7 us
    gather x3, local copies, waits for them, and re-layouts, lookup_rows(): picked = jnp.take(table, jnp.clip(local_ids, 0, own_rows - 1), axis=0)  39.2 us
    psum x1, waiting for transfers between devices, norm_adjacency(): deg_item = lax.psum(jnp.sum(mask_blk, axis=0), 'row')  33.7 us
    unnamed x11, waiting for transfers between devices  30.7 us
    all_gather x3, blocking collectives, local_fn(): user_panel = lax.all_gather(user_cur, 'col', axis=0, tiled=True)  26.8 us
    psum x1, blocking collectives, bpr_terms(): score = lax.psum(jnp.sum(e_user * (e_pos - e_neg), axis=1), 'emb')  23.3 us
  transfers between devices with their start and end apart: 8, of which 7 were waited for; matrix products, arithmetic and copies ran while one was open for 11% of the time, Pallas kernels for 0%

commit v1 on v0

v1 whole, which is shorter than its diff:
```python
import functools

import jax
import jax.numpy as jnp
from jax import lax
from jax.experimental import pallas as pl
from jax.experimental.pallas import tpu as pltpu
from jax.sharding import PartitionSpec as P

MESH = pl.DeviceIdType.MESH
F32, BF16, I32 = jnp.float32, jnp.bfloat16, jnp.int32
NUM_LAYERS = 3
CHUNK = 512


def each(lo, hi, body):
    def step(i, carry):
        body(i)
        return carry

    lax.fori_loop(lo, hi, step, 0)


def aligned(start, size, unit):
    return pl.ds(pl.multiple_of(start, unit), size)


def lane_dot(lhs, rhs):
    return lax.dot_general(lhs, rhs, (((1,), (1,)), ((), ())), preferred_element_type=F32)


def kernel(dims, mask_hbm, user_in, item_in, trip, out_user, out_item, score_out,
           mask_raw, mask_bf, adj, deg_item, deg_user, user_scale,
           user0_in, user0, item0, item1, item2,
           user1, user2, part_u, recv_u, part_i, recv_i,
           fin_tile, fin_item, item_own, fin_all, part_d, recv_d, zpart, scores,
           sem_raw, sem_one_s, sem_one_r, sem_send,
           sem_item0, sem_user0, sem_di, sem_du, sem_urs, sem_uag, sem_irs, sem_iag,
           sem_own, sem_fin, sem_d, sem_z, sem_sc):
    n_e, n_c, n_r = dims
    n_x, half = n_r // 2, n_e // 2
    n_p = n_c * n_e
    n_b = n_r * n_c
    emb, col, row = lax.axis_index("emb"), lax.axis_index("col"), lax.axis_index("row")
    chip, core = lax.div(row, 2), lax.rem(row, 2)
    rows_u = mask_hbm.shape[0]
    width = item_in.shape[1]
    sub = width // n_e
    cols = item_in.shape[0]
    kd, cu = part_u.shape[1:]
    ni = adj.shape[1]
    piece = ni // n_x
    lanes = cu // n_c
    plane = col * n_e + emb
    block = row * n_c + col
    home = lax.div(emb, half)
    in_half = lax.rem(emb, half)

    def remote(src, dst, send, recv, e, c, r):
        return pltpu.make_async_remote_copy(
            src_ref=src, dst_ref=dst, send_sem=send, recv_sem=recv, device_id=(e, c, r), device_id_type=MESH)

    def raw(i):
        return pltpu.make_async_copy(
            mask_hbm.at[:, aligned(i * width + emb * sub, sub, 128)], mask_raw.at[i], sem_raw.at[i])

    for i in range(n_r):
        raw(i).start()

    here_rows = aligned(in_half * cols, cols, 16)
    here_items = aligned(row * sub, sub, 128)
    mine = home == core

    def item0_copy(q):
        x_to, e_to = lax.div(q, n_e), lax.rem(q, n_e)
        return x_to, e_to, remote(
            item_in.at[:, aligned(e_to * sub, sub, 128)], item0.at[here_rows, here_items],
            sem_send.at[0], sem_item0.at[row * half + in_half], e_to, col, x_to * 2 + home)

    def item0_send(q):
        x_to, e_to, copy = item0_copy(q)

        @pl.when(jnp.logical_not(mine & (x_to == chip) & (e_to == emb)))
        def _():
            copy.start()

    each(0, n_x * n_e, item0_send)

    user_slot = core * n_c + col

    def user0_copy(q):
        c_to, e_to = lax.div(q, n_e), lax.rem(q, n_e)
        return c_to, e_to, remote(
            user_in, user0_in.at[user_slot, here_rows],
            sem_send.at[1], sem_user0.at[user_slot * half + in_half], e_to, c_to, chip * 2 + home)

    def user0_send(q):
        c_to, e_to, copy = user0_copy(q)

        @pl.when(jnp.logical_not(mine & (c_to == col) & (e_to == emb)))
        def _():
            copy.start()

    each(0, n_p, user0_send)

    @pl.when(mine)
    def _():
        item0[here_rows, here_items] = item_in[:, aligned(emb * sub, sub, 128)]
        user0_in[user_slot, here_rows] = user_in[...]

    own_users = aligned(core * rows_u, rows_u, 128)
    for i in range(n_r):
        raw(i).wait()
        mask_bf[own_users, i * sub:(i + 1) * sub] = mask_raw[i].astype(F32).astype(BF16)
    swap = remote(mask_bf.at[own_users], mask_bf.at[own_users], sem_one_s.at[0], sem_one_r.at[0],
                  emb, col, chip * 2 + 1 - core)
    swap.start()
    ones_u = jnp.ones((8, rows_u), BF16)
    deg_item[row] = jnp.dot(ones_u, mask_bf[own_users, :], preferred_element_type=F32)[0:1].astype(I32)

    def di_copy(j):
        r_to = lax.rem(row + j, n_r)
        return remote(deg_item.at[row], deg_item.at[row], sem_send.at[2], sem_di.at[row], emb, col, r_to)

    each(1, n_r, lambda j: di_copy(j).start())
    swap.wait_recv()
    deg_user[plane] = lane_dot(jnp.ones((8, ni), BF16), mask_bf[...])[0:1].astype(I32)

    def around(j):
        q = lax.rem(plane + j, n_p)
        return lax.div(q, n_e), lax.rem(q, n_e)

    def du_copy(j):
        c_to, e_to = around(j)
        return remote(deg_user.at[plane], deg_user.at[plane], sem_send.at[3], sem_du.at[plane], e_to, c_to, row)

    each(1, n_p, lambda j: du_copy(j).start())

    def arrived(buf, sem, slot):
        remote(buf, buf, sem_send.at[0], sem.at[slot], emb, col, row).wait_recv()

    def from_row(j):
        i = lax.rem(row + j, n_r)
        arrived(deg_item.at[i], sem_di, i)

    def from_plane(j):
        i = lax.rem(plane + j, n_p)
        arrived(deg_user.at[i], sem_du, i)

    each(1, n_r, from_row)
    each(1, n_p, from_plane)
    total_i = deg_item[0]
    for i in range(1, n_r):
        total_i = total_i + deg_item[i]
    total_u = deg_user[0]
    for i in range(1, n_p):
        total_u = total_u + deg_user[i]
    inv_item = lax.rsqrt(jnp.maximum(total_i, 1).astype(F32))
    inv_user = lax.rsqrt(jnp.maximum(total_u, 1).astype(F32))
    user_scale[...] = jnp.transpose(jnp.broadcast_to(inv_user, (128, cu)))

    def scale_rows(i):
        rs = aligned(i * 32, 32, 32)
        by_user = user_scale[rs, :]
        for j in range(ni // 128):
            js = slice(j * 128, (j + 1) * 128)
            adj[rs, js] = ((by_user * mask_bf[rs, js].astype(F32)) * inv_item[:, js]).astype(BF16)

    each(0, cu // 32, scale_rows)

    def send_part_u(k):
        def copy(j):
            c_to, e_to = around(j)
            return remote(part_u.at[k, aligned(e_to * 8, 8, 8), aligned(c_to * lanes, lanes, 128)],
                          recv_u.at[k, plane], sem_send.at[4 + k], sem_urs.at[k, plane], e_to, c_to, row)

        each(1, n_p, lambda j: copy(j).start())
        recv_u[k, plane] = part_u[k, aligned(emb * 8, 8, 8), aligned(col * lanes, lanes, 128)]

    def send_part_i(k):
        def copy(j):
            x_to = lax.rem(chip + j, n_x)
            return remote(part_i.at[k, :, aligned(x_to * piece, piece, 128)],
                          recv_i.at[k, chip], sem_send.at[7 + k], sem_irs.at[k, chip], emb, col, x_to * 2 + core)

        each(1, n_x, lambda j: copy(j).start())
        recv_i[k, chip] = part_i[k, :, aligned(chip * piece, piece, 128)]

    def sum_u(k):
        def wait(j):
            i = lax.rem(plane + j, n_p)
            arrived(recv_u.at[k, i], sem_urs.at[k], i)

        each(1, n_p, wait)
        total = recv_u[k, 0]
        for i in range(1, n_p):
            total = total + recv_u[k, i]
        return total.astype(BF16)

    def sum_i(k):
        def wait(j):
            i = lax.rem(chip + j, n_x)
            arrived(recv_i.at[k, i], sem_irs.at[k], i)

        each(1, n_x, wait)
        total = recv_i[k, 0]
        for i in range(1, n_x):
            total = total + recv_i[k, i]
        return total.astype(BF16)

    def share_u(buf, k):
        def copy(j):
            c_to, e_to = around(j)
            return remote(buf.at[plane], buf.at[plane], sem_send.at[10 + k], sem_uag.at[k, plane], e_to, c_to, row)

        each(1, n_p, lambda j: copy(j).start())

    def share_i(buf, k):
        there = aligned(chip * piece, piece, 128)

        def copy(j):
            x_to = lax.rem(chip + j, n_x)
            return remote(buf.at[:, there], buf.at[:, there], sem_send.at[12 + k], sem_iag.at[k, chip],
                          emb, col, x_to * 2 + core)

        each(1, n_x, lambda j: copy(j).start())

    def whole_u(buf, k):
        def wait(j):
            i = lax.rem(plane + j, n_p)
            arrived(buf.at[i], sem_uag.at[k], i)

        each(1, n_p, wait)
        return jnp.concatenate(
            [jnp.concatenate([buf[c * n_e + e].astype(F32) for c in range(n_c)], axis=1) for e in range(n_e)],
            axis=0).astype(BF16)

    def whole_i(buf, k):
        def wait(j):
            i = lax.rem(chip + j, n_x)
            arrived(buf.at[:, aligned(i * piece, piece, 128)], sem_iag.at[k], i)

        each(1, n_x, wait)
        return buf[...]

    def item0_wait(q):
        r_from, e_from = lax.div(q, half), lax.rem(q, half)

        @pl.when(jnp.logical_not(mine & (r_from == row) & (e_from == in_half)))
        def _():
            arrived(item0.at[aligned(e_from * cols, cols, 16), aligned(r_from * sub, sub, 128)], sem_item0, q)

    def user0_wait(q):
        s_from, e_from = lax.div(q, half), lax.rem(q, half)

        @pl.when(jnp.logical_not(mine & (s_from == user_slot) & (e_from == in_half)))
        def _():
            arrived(user0_in.at[s_from, aligned(e_from * cols, cols, 16)], sem_user0, q)

    each(0, n_r * half, item0_wait)
    each(0, 2 * n_c * half, user0_wait)
    user0[...] = jnp.concatenate(
        [user0_in[2 * t].astype(F32) + pltpu.roll(user0_in[2 * t + 1].astype(F32), lanes // 2, 1) for t in range(n_c)],
        axis=1)

    part_u[0] = lane_dot(item0[...], adj[...])
    send_part_u(0)
    part_i[0] = jnp.dot(user0[...].astype(BF16), adj[...], preferred_element_type=F32)
    send_part_i(0)

    own_items = aligned(chip * piece, piece, 128)
    own_rows, own_lanes = aligned(emb * 8, 8, 8), aligned(col * lanes, lanes, 128)
    got = sum_i(0)
    item1[:, own_items] = got
    share_i(item1, 0)
    item_acc = item0[:, own_items].astype(F32) + got.astype(F32)
    got = sum_u(0)
    user1[plane] = got
    share_u(user1, 0)
    user_acc = user0[own_rows, own_lanes] + got.astype(F32)

    part_u[1] = lane_dot(whole_i(item1, 0), adj[...])
    send_part_u(1)
    part_i[1] = jnp.dot(whole_u(user1, 0), adj[...], preferred_element_type=F32)
    send_part_i(1)
    got = sum_i(1)
    item2[:, own_items] = got
    share_i(item2, 1)
    item_acc = item_acc + got.astype(F32)
    got = sum_u(1)
    user2[plane] = got
    share_u(user2, 1)
    user_acc = user_acc + got.astype(F32)

    part_u[2] = lane_dot(whole_i(item2, 1), adj[...])
    send_part_u(2)
    part_i[2] = jnp.dot(whole_u(user2, 1), adj[...], preferred_element_type=F32)
    send_part_i(2)

    item_acc = item_acc + sum_i(2).astype(F32)
    fin_item[...] = (item_acc / (NUM_LAYERS + 1)).astype(BF16)
    back = aligned(emb * sub, sub, 128)

    def own_copy(q):
        e_to, k_to = lax.div(q, 2), lax.rem(q, 2)
        return e_to, k_to, remote(
            fin_item.at[aligned(e_to * cols, cols, 16), aligned(k_to * sub, sub, 128)], item_own.at[:, back],
            sem_send.at[14], sem_own.at[emb], half * core + e_to, col, chip * 2 + k_to)

    def own_send(q):
        e_to, k_to, copy = own_copy(q)

        @pl.when(jnp.logical_not((half * core + e_to == emb) & (k_to == core)))
        def _():
            copy.start()

    each(0, 2 * half, own_send)

    @pl.when(mine)
    def _():
        item_own[:, back] = fin_item[here_rows, aligned(core * sub, sub, 128)]

    user_acc = user_acc + sum_u(2).astype(F32)
    fin_tile[0] = (user_acc / (NUM_LAYERS + 1)).astype(BF16)
    e_fin = half * core + lax.div(emb, 2)
    top, tile = lax.rem(emb, 2), chip * n_c + col
    slot = top * (n_x * n_c) + tile

    def fin_copy(q):
        r_to, c_to = lax.div(q, n_c), lax.rem(q, n_c)
        return r_to, c_to, remote(fin_tile.at[0], fin_all.at[slot], sem_send.at[15], sem_fin.at[slot],
                                  e_fin, c_to, r_to)

    def fin_send(q):
        r_to, c_to, copy = fin_copy(q)

        @pl.when(jnp.logical_not((e_fin == emb) & (r_to == row) & (c_to == col)))
        def _():
            copy.start()

    each(0, n_b, fin_send)

    @pl.when(e_fin == emb)
    def _():
        fin_all[slot] = fin_tile[0]

    def own_wait(e_from):
        @pl.when(jnp.logical_not(mine & (e_from == emb)))
        def _():
            arrived(item_own.at[:, aligned(e_from * sub, sub, 128)], sem_own, e_from)

    each(0, n_e, own_wait)
    out_item[...] = item_own[...]

    n_hi = width // 128
    by_hi = jnp.concatenate([item_own[:, j * 128:(j + 1) * 128] for j in range(n_hi)], axis=0)
    hi_base = (col * n_r + row) * n_hi

    def pick(ids, table, first, count):
        hot = (lax.broadcasted_iota(I32, (128, ids.shape[1]), 0) == (ids & 127)).astype(F32).astype(BF16)
        found = jnp.dot(table, hot, preferred_element_type=F32)
        high = (ids >> 7) - first
        total = jnp.zeros((cols, ids.shape[1]), F32)
        for j in range(count):
            total = total + jnp.where(high == j, found[j * cols:(j + 1) * cols], 0.0)
        return total

    def pick_items(i):
        at = aligned(i * CHUNK, CHUNK, 128)
        part_d[:, at] = pick(trip[1:2, at], by_hi, hi_base, n_hi) - pick(trip[2:3, at], by_hi, hi_base, n_hi)

    each(0, trip.shape[1] // CHUNK, pick_items)

    def d_copy(j):
        q = lax.rem(block + j, n_b)
        return remote(part_d.at[:, aligned(q * 128, 128, 128)], recv_d.at[block], sem_send.at[16], sem_d.at[block],
                      emb, lax.rem(q, n_c), lax.div(q, n_c))

    each(1, n_b, lambda j: d_copy(j).start())
    recv_d[block] = part_d[:, aligned(block * 128, 128, 128)]

    def fin_wait(q):
        k_from = lax.div(emb, half)
        t_from, x_from, c_from = lax.div(q, n_x * n_c), lax.div(lax.rem(q, n_x * n_c), n_c), lax.rem(q, n_c)
        e_from = 2 * lax.rem(emb, half) + t_from

        @pl.when(jnp.logical_not(
            (k_from == core) & (x_from == chip) & (c_from == col) & (e_from == emb)))
        def _():
            arrived(fin_all.at[q], sem_fin, q)

    each(0, 2 * n_x * n_c, fin_wait)
    n_t = n_x * n_c
    here = chip * n_c + lax.div(core * n_c + col, 2)
    wide = jnp.concatenate([fin_all[here], fin_all[n_t + here]], axis=0).astype(F32)
    wide = jnp.where(lax.rem(col, 2) == 1, pltpu.roll(wide, lanes // 2, 1), wide)
    out_user[...] = wide[:, :lanes // 2].astype(BF16)
    by_tile = jnp.concatenate(
        [fin_all[s * n_t + t].astype(F32) for t in range(n_t) for s in range(2)], axis=0).astype(BF16)
    e_user = pick(trip[0:1, aligned(block * 128, 128, 128)], by_tile, 0, n_t)

    def d_wait(j):
        i = lax.rem(block + j, n_b)
        arrived(recv_d.at[i], sem_d, i)

    each(1, n_b, d_wait)
    diff = recv_d[0]
    for i in range(1, n_b):
        diff = diff + recv_d[i]
    zpart[emb] = jnp.sum(e_user * diff, axis=0, keepdims=True)

    def z_copy(j):
        return remote(zpart.at[emb], zpart.at[emb], sem_send.at[17], sem_z.at[emb], lax.rem(emb + j, n_e), col, row)

    def z_wait(j):
        i = lax.rem(emb + j, n_e)
        arrived(zpart.at[i], sem_z, i)

    each(1, n_e, lambda j: z_copy(j).start())
    each(1, n_e, z_wait)
    score = zpart[0]
    for i in range(1, n_e):
        score = score + zpart[i]
    scores[block] = score

    def s_copy(j):
        q = lax.rem(block + j, n_b)
        return remote(scores.at[block], scores.at[block], sem_send.at[18], sem_sc.at[block],
                      emb, lax.rem(q, n_c), lax.div(q, n_c))

    def s_wait(j):
        i = lax.rem(block + j, n_b)
        arrived(scores.at[i], sem_sc, i)

    each(1, n_b, lambda j: s_copy(j).start())
    each(1, n_b, s_wait)
    for i in range(n_b):
        score_out[i:i + 1, :] = scores[i]

    def left(view, i):
        remote(view, view, sem_send.at[i], sem_one_r.at[0], emb, col, row).wait_send()

    swap.wait_send()
    n_mine = jnp.where(mine, 1, 0)
    each(0, n_x * n_e - n_mine, lambda q: left(item_in.at[:, 0:sub], 0))
    each(0, n_p - n_mine, lambda q: left(user_in, 1))
    left(deg_item.at[0:n_r - 1], 2)
    left(deg_user.at[0:n_p - 1], 3)
    for k in range(3):
        left(recv_u.at[k, 0:n_p - 1], 4 + k)
        left(recv_i.at[k, 0:n_x - 1], 7 + k)
    left(user1.at[0:n_p - 1], 10)
    left(user2.at[0:n_p - 1], 11)
    left(item1.at[:, 0:piece * (n_x - 1)], 12)
    left(item2.at[:, 0:piece * (n_x - 1)], 13)
    each(0, 2 * half - n_mine, lambda q: left(item_own.at[:, 0:sub], 14))
    n_fin = n_b - jnp.where(e_fin == emb, 1, 0)
    each(0, n_fin, lambda q: left(fin_tile.at[0], 15))
    left(recv_d.at[0:n_b - 1], 16)
    left(zpart.at[0:n_e - 1], 17)
    left(scores.at[0:n_b - 1], 18)


def solution(mesh):
    dims = n_e, n_c, n_r = mesh.shape["emb"], mesh.shape["col"], mesh.shape["row"]

    def local_fn(mask_blk, user_sh, item_sh, triples):
        rows_u = mask_blk.shape[0]
        width, cols = item_sh.shape
        num_trip = triples.shape[0]
        n_x, n_p, n_b, half = n_r // 2, n_c * n_e, n_r * n_c, n_e // 2
        sub = width // n_e
        ni, cu, kd = n_r * sub, 2 * rows_u, half * cols
        piece, lanes = ni // n_x, cu // n_c
        user_t = jnp.pad(user_sh.T, ((0, 0), (0, lanes - user_sh.shape[0])))
        dma = pltpu.SemaphoreType.DMA
        vmem = pl.BlockSpec(memory_space=pltpu.VMEM)
        scratch = [
            pltpu.VMEM((n_r, rows_u, sub), I32),
            pltpu.VMEM((cu, ni), BF16),
            pltpu.VMEM((cu, ni), BF16),
            pltpu.VMEM((n_r, 1, ni), I32),
            pltpu.VMEM((n_p, 1, cu), I32),
            pltpu.VMEM((cu, 128), F32),
            pltpu.VMEM((2 * n_c, kd, lanes), BF16),
            pltpu.VMEM((kd, cu), F32),
            pltpu.VMEM((kd, ni), BF16),
            pltpu.VMEM((kd, ni), BF16),
            pltpu.VMEM((kd, ni), BF16),
            pltpu.VMEM((n_p, 8, lanes), BF16),
            pltpu.VMEM((n_p, 8, lanes), BF16),
            pltpu.VMEM((3, kd, cu), F32),
            pltpu.VMEM((3, n_p, 8, lanes), F32),
            pltpu.VMEM((3, kd, ni), F32),
            pltpu.VMEM((3, n_x, kd, piece), F32),
            pltpu.VMEM((1, 8, lanes), BF16),
            pltpu.VMEM((kd, piece), BF16),
            pltpu.VMEM((cols, width), BF16),
            pltpu.VMEM((2 * n_x * n_c, 8, lanes), BF16),
            pltpu.VMEM((cols, num_trip), F32),
            pltpu.VMEM((n_b, cols, 128), F32),
            pltpu.VMEM((n_e, 1, 128), F32),
            pltpu.VMEM((n_b, 1, 128), F32),
            dma((n_r,)), dma((1,)), dma((1,)), dma((19,)),
            dma((n_r * half,)), dma((2 * n_c * half,)), dma((n_r,)), dma((n_p,)),
            dma((3, n_p)), dma((2, n_p)), dma((3, n_x)), dma((2, n_x)),
            dma((n_e,)), dma((2 * n_x * n_c,)), dma((n_b,)), dma((n_e,)), dma((n_b,)),
        ]
        user_t, item_t, score = pl.pallas_call(
            functools.partial(kernel, dims),
            out_shape=(jax.ShapeDtypeStruct((cols, user_sh.shape[0]), BF16),
                       jax.ShapeDtypeStruct((cols, width), BF16),
                       jax.ShapeDtypeStruct((n_b, 128), F32)),
            in_specs=[pl.BlockSpec(memory_space=pl.ANY), vmem, vmem, vmem],
            out_specs=(vmem, vmem, vmem),
            scratch_shapes=scratch,
            compiler_params=pltpu.CompilerParams(has_side_effects=True, vmem_limit_bytes=48 << 20),
        )(mask_blk, user_t, item_sh.T, triples.T)
        return user_t.T, item_t.T, jax.nn.softplus(-score.reshape(num_trip))

    return jax.shard_map(
        local_fn, mesh=mesh,
        in_specs=(P("row", "col"), P(("row", "col"), "emb"), P(("col", "row"), "emb"), P()),
        out_specs=(P(("row", "col"), "emb"), P(("col", "row"), "emb"), P()),
        check_vma=False)
```

time: 505 us -> 106 us (0.21); the launches traced: 497 us -> 106 us
  waiting for transfers between devices: 263 us -> 0 us
  blocking collectives: 106 us -> 0 us
  Pallas kernels: 0 us -> 101 us
  local copies, waits for them, and re-layouts: 49.6 us -> 3.59 us
  matrix products: 32.6 us -> 0 us
  other arithmetic: 31.4 us -> 0.63 us
  between operations: 14.4 us -> 0.64 us
    psum x2 -> x0, waiting for transfers between devices: 148 us -> none  [the longest x1 114 us: bpr_terms(): fetched = lax.psum(fetched, ('row', 'col'))]
    pallas_call x0 -> x1, Pallas kernels: none -> 101 us  [local_fn(): pl.pallas_call(functools.partial(kernel, dims), out_shape=(jax.ShapeDtype...]
    reduce_scatter x3 -> x0, waiting for transfers between devices: 84.4 us -> none  [local_fn(): lax.psum_scatter(item_part, 'row', scatter_dimension=0, tiled=True)]
    all_gather x6 -> x0, blocking collectives: 74.5 us -> none  [the longest x3 47.7 us: local_fn(): item_panel = lax.all_gather(item_cur, 'row', axis=0, tiled=True)]
    gather x3 -> x0, local copies, waits for them, and re-layouts: 39.2 us -> none  [lookup_rows(): picked = jnp.take(table, jnp.clip(local_ids, 0, own_rows - 1), axis=0)]
    psum x2 -> x0, blocking collectives: 31.2 us -> none  [the longest x1 23.3 us: bpr_terms(): score = lax.psum(jnp.sum(e_user * (e_pos - e_neg), axis=1), 'emb')]
    unnamed x11 -> x0, waiting for transfers between devices: 30.7 us -> none
    dot_general x3 -> x0, matrix products: 16.9 us -> none  [local_fn(): lax.dot_general(adj_blk, user_panel, (((0,), (0,)), ((), ())), preferred_...]
  transfers between devices with their start and end apart: 8 -> 0, of which waited for: 7 -> 0; matrix products, arithmetic and copies ran while one was open for 11% -> 0% of each run, Pallas kernels for 0% -> 0%
where the time goes in v1:
time: 106 us
  Pallas kernels  101 us (95%)
  local copies, waits for them, and re-layouts  3.59 us (3%)
    pallas_call x1, Pallas kernels, local_fn(): pl.pallas_call(functools.partial(kernel, dims), out_shape=(jax.ShapeDtype...  101 us
    unnamed x6, local copies, waits for them, and re-layouts  2.9 us

profile of v1, /device:TPU:1, one launch (start us, length us, event | category | flops | bytes accessed | tf_op | source)
XLA Modules:
  0.0 105.6 jit_solution(2436123244899476768)
XLA Ops:
  0.6 0.7 pad.4.user_in
  1.3 0.0 copy-start
  1.3 0.8 copy-done
  2.2 0.0 copy-start.1
  2.2 0.8 copy-done.1
  3.0 100.7 %shard_map.67 = (bf16[16,64]{1,0:T(8,128)(2,1)S(1)}, bf16[16,2048]{1,0:T(8,128)(2,1)S(1)}, f32[32,128]{1,0:T(8,128)S(1)}) custom-call(s32[256,16384]{1,0:T(8,128)} %mask_hbm.1, bf16[16,128]{1,0:T(8,128)(2,1)S(1)} %pad.4.user_in, bf16[16,2048]{1,0:T(8,128)(2,1)S(1)} %bitcast.21, s32[3,4096]{1,0:T(4,128)S(1)} %bitcast.22), custom_call_target="tpu_custom_call" | custom-call | tf_op jit(solution)/shard_map/pallas_call | solution.py:509
  103.7 0.6 compare_select_fusion
  104.4 0.6 copy.9
  105.0 0.6 copy.10
Async XLA Ops:
  1.3 0.8 copy-start
  2.2 0.8 copy-start.1

commit v2 on v1

--- a/solution.py
+++ b/solution.py
@@ -29,12 +29,12 @@
     return lax.dot_general(lhs, rhs, (((1,), (1,)), ((), ())), preferred_element_type=F32)
 
 
-def kernel(dims, mask_hbm, user_in, item_in, trip, out_user, out_item, score_out,
-           mask_raw, mask_bf, adj, deg_item, deg_user, user_scale,
+def kernel(dims, mask_hbm, user_hbm, item_hbm, trip_hbm, out_user, out_item, score_out,
+           user_in, user_pack, user_wide, item_in, trip, mask_raw, mask_bf, adj, deg_item, deg_user, user_scale,
            user0_in, user0, item0, item1, item2,
            user1, user2, part_u, recv_u, part_i, recv_i,
            fin_tile, fin_item, item_own, fin_all, part_d, recv_d, zpart, scores,
-           sem_raw, sem_one_s, sem_one_r, sem_send,
+           sem_raw, sem_in, sem_one_s, sem_one_r, sem_send,
            sem_item0, sem_user0, sem_di, sem_du, sem_urs, sem_uag, sem_irs, sem_iag,
            sem_own, sem_fin, sem_d, sem_z, sem_sc):
     n_e, n_c, n_r = dims
@@ -64,12 +64,89 @@
         return pltpu.make_async_copy(
             mask_hbm.at[:, aligned(i * width + emb * sub, sub, 128)], mask_raw.at[i], sem_raw.at[i])
 
+    fetch = [pltpu.make_async_copy(src, dst, sem_in.at[i]) for i, (src, dst) in enumerate(
+        ((user_hbm, user_in), (item_hbm, item_in), (trip_hbm, trip)))]
     for i in range(n_r):
         raw(i).start()
+    for copy in fetch:
+        copy.start()
+
+    barrier = pltpu.get_barrier_semaphore()
+
+    def hello(e, c, r):
+        pl.semaphore_signal(barrier, inc=1, device_id=(e, c, r), device_id_type=MESH)
+
+    def hello_col(j):
+        q = lax.rem(row * n_e + emb + j, n_r * n_e)
+        hello(lax.rem(q, n_e), col, lax.div(q, n_e))
+
+    def hello_chip(j):
+        c_to, left_over = lax.rem(col + 1 + lax.div(j, 2 * n_e), n_c), lax.rem(j, 2 * n_e)
+        hello(lax.div(left_over, 2), c_to, chip * 2 + lax.rem(left_over, 2))
+
+    each(1, n_r * n_e, hello_col)
+    each(0, 2 * n_e * (n_c - 1), hello_chip)
+
+    own_users = aligned(core * rows_u, rows_u, 128)
+    for i in range(n_r):
+        raw(i).wait()
+        mask_bf[own_users, i * sub:(i + 1) * sub] = mask_raw[i].astype(F32).astype(BF16)
+    own_mask = mask_bf[own_users, :]
+    deg_item[row] = jnp.dot(jnp.ones((8, rows_u), BF16), own_mask, preferred_element_type=F32)[0:1].astype(I32)
+    own_part = core * n_p + plane
+    deg_user[own_part] = lane_dot(jnp.ones((8, ni), BF16), own_mask)[0:1].astype(I32)
+
+    fetch[0].wait()
+    user_wide[...] = jnp.zeros_like(user_wide)
+    user_wide[:, 0:lanes // 2] = user_in[...].astype(F32)
+    wide = user_wide[...]
+    user_pack[...] = (wide[0:8] + pltpu.roll(wide[8:16], lanes // 2, 1)).astype(BF16)
+    fetch[1].wait()
+    fetch[2].wait()
+    pl.semaphore_wait(barrier, n_r * n_e - 1 + 2 * n_e * (n_c - 1))
+
+    swap = remote(mask_bf.at[own_users], mask_bf.at[own_users], sem_one_s.at[0], sem_one_r.at[0],
+                  emb, col, chip * 2 + 1 - core)
+    swap.start()
+
+    def di_copy(j):
+        r_to = lax.rem(row + j, n_r)
+        return remote(deg_item.at[row], deg_item.at[row], sem_send.at[2], sem_di.at[row], emb, col, r_to)
+
+    each(1, n_r, lambda j: di_copy(j).start())
+
+    def around(j):
+        q = lax.rem(plane + j, n_p)
+        return lax.div(q, n_e), lax.rem(q, n_e)
+
+    def du_copy(j):
+        q = lax.rem(own_part + j, 2 * n_p)
+        k_to, p_to = lax.div(q, n_p), lax.rem(q, n_p)
+        return remote(deg_user.at[own_part], deg_user.at[own_part], sem_send.at[3], sem_du.at[own_part],
+                      lax.rem(p_to, n_e), lax.div(p_to, n_e), chip * 2 + k_to)
+
+    each(1, 2 * n_p, lambda j: du_copy(j).start())
 
     here_rows = aligned(in_half * cols, cols, 16)
     here_items = aligned(row * sub, sub, 128)
     mine = home == core
+
+    user_slot = (core * n_c + col) * half + in_half
+
+    def user0_copy(q):
+        c_to, e_to = lax.div(q, n_e), lax.rem(q, n_e)
+        return c_to, e_to, remote(user_pack, user0_in.at[user_slot], sem_send.at[1], sem_user0.at[user_slot],
+                                  e_to, c_to, chip * 2 + home)
+
+    def user0_send(q):
+        c_to, e_to, copy = user0_copy(q)
+
+        @pl.when(jnp.logical_not(mine & (c_to == col) & (e_to == emb)))
+        def _():
+            copy.start()
+
+    each(0, n_p, user0_send)
+
 
     def item0_copy(q):
         x_to, e_to = lax.div(q, n_e), lax.rem(q, n_e)
@@ -86,55 +163,10 @@
 
     each(0, n_x * n_e, item0_send)
 
-    user_slot = core * n_c + col
-
-    def user0_copy(q):
-        c_to, e_to = lax.div(q, n_e), lax.rem(q, n_e)
-        return c_to, e_to, remote(
-            user_in, user0_in.at[user_slot, here_rows],
-            sem_send.at[1], sem_user0.at[user_slot * half + in_half], e_to, c_to, chip * 2 + home)
-
-    def user0_send(q):
-        c_to, e_to, copy = user0_copy(q)
-
-        @pl.when(jnp.logical_not(mine & (c_to == col) & (e_to == emb)))
-        def _():
-            copy.start()
-
-    each(0, n_p, user0_send)
-
     @pl.when(mine)
     def _():
         item0[here_rows, here_items] = item_in[:, aligned(emb * sub, sub, 128)]
-        user0_in[user_slot, here_rows] = user_in[...]
-
-    own_users = aligned(core * rows_u, rows_u, 128)
-    for i in range(n_r):
-        raw(i).wait()
-        mask_bf[own_users, i * sub:(i + 1) * sub] = mask_raw[i].astype(F32).astype(BF16)
-    swap = remote(mask_bf.at[own_users], mask_bf.at[own_users], sem_one_s.at[0], sem_one_r.at[0],
-                  emb, col, chip * 2 + 1 - core)
-    swap.start()
-    ones_u = jnp.ones((8, rows_u), BF16)
-    deg_item[row] = jnp.dot(ones_u, mask_bf[own_users, :], preferred_element_type=F32)[0:1].astype(I32)
-
-    def di_copy(j):
-        r_to = lax.rem(row + j, n_r)
-        return remote(deg_item.at[row], deg_item.at[row], sem_send.at[2], sem_di.at[row], emb, col, r_to)
-
-    each(1, n_r, lambda j: di_copy(j).start())
-    swap.wait_recv()
-    deg_user[plane] = lane_dot(jnp.ones((8, ni), BF16), mask_bf[...])[0:1].astype(I32)
-
-    def around(j):
-        q = lax.rem(plane + j, n_p)
-        return lax.div(q, n_e), lax.rem(q, n_e)
-
-    def du_copy(j):
-        c_to, e_to = around(j)
-        return remote(deg_user.at[plane], deg_user.at[plane], sem_send.at[3], sem_du.at[plane], e_to, c_to, row)
-
-    each(1, n_p, lambda j: du_copy(j).start())
+        user0_in[user_slot] = user_pack[...]
 
     def arrived(buf, sem, slot):
         remote(buf, buf, sem_send.at[0], sem.at[slot], emb, col, row).wait_recv()
@@ -144,17 +176,21 @@
         arrived(deg_item.at[i], sem_di, i)
 
     def from_plane(j):
-        i = lax.rem(plane + j, n_p)
+        i = lax.rem(own_part + j, 2 * n_p)
         arrived(deg_user.at[i], sem_du, i)
 
     each(1, n_r, from_row)
-    each(1, n_p, from_plane)
+    each(1, 2 * n_p, from_plane)
     total_i = deg_item[0]
     for i in range(1, n_r):
         total_i = total_i + deg_item[i]
-    total_u = deg_user[0]
-    for i in range(1, n_p):
-        total_u = total_u + deg_user[i]
+    totals = []
+    for k in range(2):
+        total = deg_user[k * n_p]
+        for i in range(1, n_p):
+            total = total + deg_user[k * n_p + i]
+        totals.append(total)
+    total_u = jnp.concatenate(totals, axis=1)
     inv_item = lax.rsqrt(jnp.maximum(total_i, 1).astype(F32))
     inv_user = lax.rsqrt(jnp.maximum(total_u, 1).astype(F32))
     user_scale[...] = jnp.transpose(jnp.broadcast_to(inv_user, (128, cu)))
@@ -166,6 +202,7 @@
             js = slice(j * 128, (j + 1) * 128)
             adj[rs, js] = ((by_user * mask_bf[rs, js].astype(F32)) * inv_item[:, js]).astype(BF16)
 
+    swap.wait_recv()
     each(0, cu // 32, scale_rows)
 
     def send_part_u(k):
@@ -251,22 +288,25 @@
             arrived(item0.at[aligned(e_from * cols, cols, 16), aligned(r_from * sub, sub, 128)], sem_item0, q)
 
     def user0_wait(q):
-        s_from, e_from = lax.div(q, half), lax.rem(q, half)
-
-        @pl.when(jnp.logical_not(mine & (s_from == user_slot) & (e_from == in_half)))
-        def _():
-            arrived(user0_in.at[s_from, aligned(e_from * cols, cols, 16)], sem_user0, q)
-
+        @pl.when(jnp.logical_not(mine & (q == user_slot)))
+        def _():
+            arrived(user0_in.at[q], sem_user0, q)
+
+    each(0, 2 * n_c * half, user0_wait)
+    low = lax.broadcasted_iota(I32, (8, lanes), 1) < lanes // 2
+    for t in range(n_c):
+        for i in range(half):
+            one = user0_in[2 * t * half + i].astype(F32)
+            two = user0_in[(2 * t + 1) * half + i].astype(F32)
+            ts = slice(t * lanes, (t + 1) * lanes)
+            user0[i * cols:i * cols + 8, ts] = jnp.where(low, one, pltpu.roll(two, lanes // 2, 1))
+            user0[i * cols + 8:i * cols + 16, ts] = jnp.where(low, pltpu.roll(one, lanes // 2, 1), two)
+
+    part_i[0] = jnp.dot(user0[...].astype(BF16), adj[...], preferred_element_type=F32)
+    send_part_i(0)
     each(0, n_r * half, item0_wait)
-    each(0, 2 * n_c * half, user0_wait)
-    user0[...] = jnp.concatenate(
-        [user0_in[2 * t].astype(F32) + pltpu.roll(user0_in[2 * t + 1].astype(F32), lanes // 2, 1) for t in range(n_c)],
-        axis=1)
-
     part_u[0] = lane_dot(item0[...], adj[...])
     send_part_u(0)
-    part_i[0] = jnp.dot(user0[...].astype(BF16), adj[...], preferred_element_type=F32)
-    send_part_i(0)
 
     own_items = aligned(chip * piece, piece, 128)
     own_rows, own_lanes = aligned(emb * 8, 8, 8), aligned(col * lanes, lanes, 128)
@@ -283,19 +323,19 @@
     send_part_u(1)
     part_i[1] = jnp.dot(whole_u(user1, 0), adj[...], preferred_element_type=F32)
     send_part_i(1)
+    got = sum_u(1)
+    user2[plane] = got
+    share_u(user2, 1)
+    user_acc = user_acc + got.astype(F32)
     got = sum_i(1)
     item2[:, own_items] = got
     share_i(item2, 1)
     item_acc = item_acc + got.astype(F32)
-    got = sum_u(1)
-    user2[plane] = got
-    share_u(user2, 1)
-    user_acc = user_acc + got.astype(F32)
-
+
+    part_i[2] = jnp.dot(whole_u(user2, 1), adj[...], preferred_element_type=F32)
+    send_part_i(2)
     part_u[2] = lane_dot(whole_i(item2, 1), adj[...])
     send_part_u(2)
-    part_i[2] = jnp.dot(whole_u(user2, 1), adj[...], preferred_element_type=F32)
-    send_part_i(2)
 
     item_acc = item_acc + sum_i(2).astype(F32)
     fin_item[...] = (item_acc / (NUM_LAYERS + 1)).astype(BF16)
@@ -365,18 +405,22 @@
             total = total + jnp.where(high == j, found[j * cols:(j + 1) * cols], 0.0)
         return total
 
+    n_chunk, per_chunk = trip.shape[1] // CHUNK, CHUNK // 128
+
+    def d_send(q):
+        @pl.when(q != block)
+        def _():
+            remote(part_d.at[:, aligned(q * 128, 128, 128)], recv_d.at[block], sem_send.at[16], sem_d.at[block],
+                   emb, lax.rem(q, n_c), lax.div(q, n_c)).start()
+
     def pick_items(i):
-        at = aligned(i * CHUNK, CHUNK, 128)
+        chunk = lax.rem(lax.div(block, per_chunk) + i, n_chunk)
+        at = aligned(chunk * CHUNK, CHUNK, 128)
         part_d[:, at] = pick(trip[1:2, at], by_hi, hi_base, n_hi) - pick(trip[2:3, at], by_hi, hi_base, n_hi)
-
-    each(0, trip.shape[1] // CHUNK, pick_items)
-
-    def d_copy(j):
-        q = lax.rem(block + j, n_b)
-        return remote(part_d.at[:, aligned(q * 128, 128, 128)], recv_d.at[block], sem_send.at[16], sem_d.at[block],
-                      emb, lax.rem(q, n_c), lax.div(q, n_c))
-
-    each(1, n_b, lambda j: d_copy(j).start())
+        for j in range(per_chunk):
+            d_send(chunk * per_chunk + j)
+
+    each(0, n_chunk, pick_items)
     recv_d[block] = part_d[:, aligned(block * 128, 128, 128)]
 
     def fin_wait(q):
@@ -417,25 +461,6 @@
         arrived(zpart.at[i], sem_z, i)
 
     each(1, n_e, lambda j: z_copy(j).start())
-    each(1, n_e, z_wait)
-    score = zpart[0]
-    for i in range(1, n_e):
-        score = score + zpart[i]
-    scores[block] = score
-
-    def s_copy(j):
-        q = lax.rem(block + j, n_b)
-        return remote(scores.at[block], scores.at[block], sem_send.at[18], sem_sc.at[block],
-                      emb, lax.rem(q, n_c), lax.div(q, n_c))
-
-    def s_wait(j):
-        i = lax.rem(block + j, n_b)
-        arrived(scores.at[i], sem_sc, i)
-
-    each(1, n_b, lambda j: s_copy(j).start())
-    each(1, n_b, s_wait)
-    for i in range(n_b):
-        score_out[i:i + 1, :] = scores[i]
 
     def left(view, i):
         remote(view, view, sem_send.at[i], sem_one_r.at[0], emb, col, row).wait_send()
@@ -443,9 +468,9 @@
     swap.wait_send()
     n_mine = jnp.where(mine, 1, 0)
     each(0, n_x * n_e - n_mine, lambda q: left(item_in.at[:, 0:sub], 0))
-    each(0, n_p - n_mine, lambda q: left(user_in, 1))
+    each(0, n_p - n_mine, lambda q: left(user_pack, 1))
     left(deg_item.at[0:n_r - 1], 2)
-    left(deg_user.at[0:n_p - 1], 3)
+    left(deg_user.at[0:2 * n_p - 1], 3)
     for k in range(3):
         left(recv_u.at[k, 0:n_p - 1], 4 + k)
         left(recv_i.at[k, 0:n_x - 1], 7 + k)
@@ -457,6 +482,26 @@
     n_fin = n_b - jnp.where(e_fin == emb, 1, 0)
     each(0, n_fin, lambda q: left(fin_tile.at[0], 15))
     left(recv_d.at[0:n_b - 1], 16)
+
+    each(1, n_e, z_wait)
+    score = zpart[0]
+    for i in range(1, n_e):
+        score = score + zpart[i]
+    scores[block] = score
+
+    def s_copy(j):
+        q = lax.rem(block + j, n_b)
+        return remote(scores.at[block], scores.at[block], sem_send.at[18], sem_sc.at[block],
+                      emb, lax.rem(q, n_c), lax.div(q, n_c))
+
+    def s_wait(j):
+        i = lax.rem(block + j, n_b)
+        arrived(scores.at[i], sem_sc, i)
+
+    each(1, n_b, lambda j: s_copy(j).start())
+    each(1, n_b, s_wait)
+    for i in range(n_b):
+        score_out[i:i + 1, :] = scores[i]
     left(zpart.at[0:n_e - 1], 17)
     left(scores.at[0:n_b - 1], 18)
 
@@ -472,17 +517,21 @@
         sub = width // n_e
         ni, cu, kd = n_r * sub, 2 * rows_u, half * cols
         piece, lanes = ni // n_x, cu // n_c
-        user_t = jnp.pad(user_sh.T, ((0, 0), (0, lanes - user_sh.shape[0])))
         dma = pltpu.SemaphoreType.DMA
-        vmem = pl.BlockSpec(memory_space=pltpu.VMEM)
+        vmem, hbm = pl.BlockSpec(memory_space=pltpu.VMEM), pl.BlockSpec(memory_space=pl.ANY)
         scratch = [
+            pltpu.VMEM((cols, user_sh.shape[0]), BF16),
+            pltpu.VMEM((8, lanes), BF16),
+            pltpu.VMEM((cols, lanes), F32),
+            pltpu.VMEM((cols, width), BF16),
+            pltpu.VMEM((3, num_trip), I32),
             pltpu.VMEM((n_r, rows_u, sub), I32),
             pltpu.VMEM((cu, ni), BF16),
             pltpu.VMEM((cu, ni), BF16),
             pltpu.VMEM((n_r, 1, ni), I32),
-            pltpu.VMEM((n_p, 1, cu), I32),
+            pltpu.VMEM((2 * n_p, 1, rows_u), I32),
             pltpu.VMEM((cu, 128), F32),
-            pltpu.VMEM((2 * n_c, kd, lanes), BF16),
+            pltpu.VMEM((2 * n_c * half, 8, lanes), BF16),
             pltpu.VMEM((kd, cu), F32),
             pltpu.VMEM((kd, ni), BF16),
             pltpu.VMEM((kd, ni), BF16),
@@ -501,8 +550,8 @@
             pltpu.VMEM((n_b, cols, 128), F32),
             pltpu.VMEM((n_e, 1, 128), F32),
             pltpu.VMEM((n_b, 1, 128), F32),
-            dma((n_r,)), dma((1,)), dma((1,)), dma((19,)),
-            dma((n_r * half,)), dma((2 * n_c * half,)), dma((n_r,)), dma((n_p,)),
+            dma((n_r,)), dma((3,)), dma((1,)), dma((1,)), dma((19,)),
+            dma((n_r * half,)), dma((2 * n_c * half,)), dma((n_r,)), dma((2 * n_p,)),
             dma((3, n_p)), dma((2, n_p)), dma((3, n_x)), dma((2, n_x)),
             dma((n_e,)), dma((2 * n_x * n_c,)), dma((n_b,)), dma((n_e,)), dma((n_b,)),
         ]
@@ -511,11 +560,11 @@
             out_shape=(jax.ShapeDtypeStruct((cols, user_sh.shape[0]), BF16),
                        jax.ShapeDtypeStruct((cols, width), BF16),
                        jax.ShapeDtypeStruct((n_b, 128), F32)),
-            in_specs=[pl.BlockSpec(memory_space=pl.ANY), vmem, vmem, vmem],
+            in_specs=[hbm, hbm, hbm, hbm],
             out_specs=(vmem, vmem, vmem),
             scratch_shapes=scratch,
-            compiler_params=pltpu.CompilerParams(has_side_effects=True, vmem_limit_bytes=48 << 20),
-        )(mask_blk, user_t, item_sh.T, triples.T)
+            compiler_params=pltpu.CompilerParams(collective_id=0, has_side_effects=True, vmem_limit_bytes=48 << 20),
+        )(mask_blk, user_sh.T, item_sh.T, triples.T)
         return user_t.T, item_t.T, jax.nn.softplus(-score.reshape(num_trip))
 
     return jax.shard_map(

time: 106 us -> 89.7 us (0.85)
  Pallas kernels: 101 us -> 84.7 us
    pallas_call x1, Pallas kernels: 101 us -> 84.7 us  [local_fn(): pl.pallas_call(functools.partial(kernel, dims), out_shape=(jax.ShapeDtype...]
    unnamed x6 -> x8, local copies, waits for them, and re-layouts: 2.9 us -> 3.58 us
where the time goes in v2:
time: 89.7 us; the launch traced here: 89.5 us
  Pallas kernels  84.7 us (94%)
  local copies, waits for them, and re-layouts  3.58 us (4%)
    pallas_call x1, Pallas kernels, local_fn(): pl.pallas_call(functools.partial(kernel, dims), out_shape=(jax.ShapeDtype...  84.7 us
    unnamed x8, local copies, waits for them, and re-layouts  3.58 us

profile of v2, /device:TPU:1, one launch (start us, length us, event | category | flops | bytes accessed | tf_op | source)
XLA Modules:
  0.0 89.5 jit_solution(11481252235348226619)
XLA Ops:
  0.6 0.0 copy-start
  0.6 0.8 copy-done
  1.5 0.0 copy-start.1
  1.5 0.8 copy-done.1
  2.3 0.0 copy-start.2
  2.3 0.7 copy-done.2
  3.0 84.7 %shard_map.67 = (bf16[16,64]{1,0:T(8,128)(2,1)S(1)}, bf16[16,2048]{1,0:T(8,128)(2,1)S(1)}, f32[32,128]{1,0:T(8,128)S(1)}) custom-call(s32[256,16384]{1,0:T(8,128)} %mask_hbm.1, bf16[16,64]{1,0:T(8,128)(2,1)S(1)} %bitcast.24, bf16[16,2048]{1,0:T(8,128)(2,1)S(1)} %bitcast.21, s32[3,4096]{1,0:T(4,128)S(1)} %bitcast.22), custom_call_target="tpu_custom_call" | custom-call | tf_op jit(solution)/shard_map/pallas_call | solution.py:558
  87.7 0.6 compare_select_fusion
  88.3 0.6 copy.9
  88.9 0.6 copy.10
Async XLA Ops:
  0.6 0.8 copy-start
  1.5 0.8 copy-start.1
  2.3 0.7 copy-start.2

commit v3 on v2

v3 whole, which is shorter than its diff:
```python
import functools

import jax
import jax.numpy as jnp
from jax import lax
from jax.experimental import pallas as pl
from jax.experimental.pallas import tpu as pltpu
from jax.sharding import PartitionSpec as P

MESH = pl.DeviceIdType.MESH
F32, BF16, I32 = jnp.float32, jnp.bfloat16, jnp.int32
NUM_LAYERS = 3
CHUNK = 512
LOW = 256


def each(lo, hi, body):
    def step(i, carry):
        body(i)
        return carry

    lax.fori_loop(lo, hi, step, 0)


def aligned(start, size, unit):
    return pl.ds(pl.multiple_of(start, unit), size)


def lane_dot(lhs, rhs):
    return lax.dot_general(lhs, rhs, (((1,), (1,)), ((), ())), preferred_element_type=F32)


def far_first(*sizes):
    offsets = [()]
    for n in sizes:
        offsets = [(*o, i) for o in offsets for i in range(n)]
    return sorted(offsets, key=lambda o: -sum(min(i, n - i) for i, n in zip(o, sizes)))


def others(*sizes):
    offsets = [()]
    for n in sizes:
        offsets = [(*o, i) for o in offsets for i in range(n)]
    return offsets[1:]


(S_ITEM0, S_USER0, S_DI, S_DU, S_RU, S_RI, S_GU, S_GI, S_OWN, S_FIN, S_D, S_Z, S_S, S_SWAP, NUM_SEMS) = (
    0, 1, 2, 3, 4, 7, 10, 12, 14, 15, 16, 17, 18, 19, 20)


def kernel(dims, mask_hbm, user_hbm, item_hbm, trip_hbm, out_user, out_item, score_out,
           user_in, user_pack, user_wide, item_in, trip, mask_raw, row_acc, mask_bf, adj, deg_item, deg_user, user_scale,
           user0_in, user0, item0, item1, item2,
           user1, user2, part_u, recv_u, part_i, recv_i,
           fin_tile, fin_item, item_own, fin_all, hot_item, part_d, recv_d, zpart, scores,
           sem_raw, sem_in, sem_send, sem_recv):
    n_e, n_c, n_r = dims
    n_x, half = n_r // 2, n_e // 2
    n_p = n_c * n_e
    n_b = n_r * n_c
    emb, col, row = lax.axis_index("emb"), lax.axis_index("col"), lax.axis_index("row")
    chip, core = lax.div(row, 2), lax.rem(row, 2)
    rows_u = mask_hbm.shape[0]
    width = item_in.shape[1]
    sub = width // n_e
    cols = item_in.shape[0]
    kd, cu = part_u.shape[1:]
    ni = adj.shape[1]
    piece = ni // n_x
    lanes = cu // n_c
    plane = col * n_e + emb
    block = row * n_c + col
    home = lax.div(emb, half)
    in_half = lax.rem(emb, half)
    mine = home == core
    e_at = [lax.rem(emb + i, n_e) for i in range(n_e)]
    c_at = [lax.rem(col + i, n_c) for i in range(n_c)]
    x_at = [lax.rem(chip + i, n_x) for i in range(n_x)]
    k_at = [core, 1 - core]

    def remote(src, dst, stage, e, c, r):
        return pltpu.make_async_remote_copy(
            src_ref=src, dst_ref=dst, send_sem=sem_send.at[stage], recv_sem=sem_recv.at[stage],
            device_id=(e, c, r), device_id_type=MESH)

    def arrived(view, stage):
        remote(view, view, stage, emb, col, row).wait_recv()

    def left(view, stage):
        remote(view, view, stage, emb, col, row).wait_send()

    def either(wait, alone, less, full, stage):
        @pl.when(alone)
        def _():
            wait(less, stage)

        @pl.when(jnp.logical_not(alone))
        def _():
            wait(full, stage)

    def raw(i):
        return pltpu.make_async_copy(
            mask_hbm.at[:, i * width:(i + 1) * width], mask_raw.at[i], sem_raw.at[i])

    fetch = [pltpu.make_async_copy(src, dst, sem_in.at[i]) for i, (src, dst) in enumerate(
        ((user_hbm, user_in), (item_hbm, item_in), (trip_hbm, trip)))]

    barrier = pltpu.get_barrier_semaphore()

    def hello(e, c, r):
        pl.semaphore_signal(barrier, inc=1, device_id=(e, c, r), device_id_type=MESH)

    for x_o, e_o, k_o in far_first(n_x, n_e, 2)[:-1]:
        hello(e_at[e_o], col, x_at[x_o] * 2 + k_at[k_o])
    for c_o, e_o, k_o in far_first(n_c, n_e, 2):
        if c_o:
            hello(e_at[e_o], c_at[c_o], chip * 2 + k_at[k_o])
    for i in range(n_r):
        raw(i).start()
    for copy in fetch:
        copy.start()

    own_users = aligned(core * rows_u, rows_u, 128)
    at_emb = aligned(emb * sub, sub, 128)
    for i in range(n_r):
        raw(i).wait()
        mask_bf[own_users, i * sub:(i + 1) * sub] = mask_raw[i, :, at_emb].astype(F32).astype(BF16)

        def row_sums(t):
            rs = aligned(t * 32, 32, 32)
            total = mask_raw[i, rs, 0:128]
            for j in range(1, width // 128):
                total = total + mask_raw[i, rs, j * 128:(j + 1) * 128]
            row_acc[rs, :] = total if i == 0 else row_acc[rs, :] + total

        each(0, rows_u // 32, row_sums)
    own_mask = mask_bf[own_users, :]
    deg_item[row] = jnp.dot(jnp.ones((8, rows_u), BF16), own_mask, preferred_element_type=F32)[0:1].astype(I32)
    own_part = core * n_c + col
    deg_user[own_part] = jnp.sum(jnp.transpose(row_acc[...].astype(F32)), axis=0, keepdims=True).astype(I32)

    fetch[0].wait()
    user_wide[...] = jnp.zeros_like(user_wide)
    user_wide[:, 0:lanes // 2] = user_in[...].astype(F32)
    wide = user_wide[...]
    user_pack[...] = (wide[0:8] + pltpu.roll(wide[8:16], lanes // 2, 1)).astype(BF16)
    fetch[1].wait()
    fetch[2].wait()
    pl.semaphore_wait(barrier, n_r * n_e - 1 + 2 * n_e * (n_c - 1))

    for c_o, k_o in others(n_c, 2):
        remote(deg_user.at[own_part], deg_user.at[own_part], S_DU, emb, c_at[c_o], chip * 2 + k_at[k_o]).start()
    for x_o, k_o in others(n_x, 2):
        remote(deg_item.at[row], deg_item.at[row], S_DI, emb, col, x_at[x_o] * 2 + k_at[k_o]).start()

    here_rows = aligned(in_half * cols, cols, 16)
    here_items = aligned(row * sub, sub, 128)
    user_slot = (core * n_c + col) * half + in_half

    def user0_send(c_o, e_o):
        remote(user_pack, user0_in.at[user_slot], S_USER0, e_at[e_o], c_at[c_o], chip * 2 + home).start()

    for c_o, e_o in others(n_c, n_e):
        user0_send(c_o, e_o)
    remote(mask_bf.at[own_users], mask_bf.at[own_users], S_SWAP, emb, col, chip * 2 + 1 - core).start()

    def item0_send(x_o, e_o):
        remote(item_in.at[:, aligned(e_at[e_o] * sub, sub, 128)], item0.at[here_rows, here_items], S_ITEM0,
               e_at[e_o], col, x_at[x_o] * 2 + home).start()

    for x_o, e_o in others(n_x, n_e):
        item0_send(x_o, e_o)

    @pl.when(jnp.logical_not(mine))
    def _():
        user0_send(0, 0)
        item0_send(0, 0)

    @pl.when(mine)
    def _():
        item0[here_rows, here_items] = item_in[:, aligned(emb * sub, sub, 128)]
        user0_in[user_slot] = user_pack[...]

    arrived(deg_item.at[0:n_r - 1], S_DI)
    arrived(deg_user.at[0:2 * n_c - 1], S_DU)
    total_i = deg_item[0]
    for i in range(1, n_r):
        total_i = total_i + deg_item[i]
    totals = []
    for k in range(2):
        total = deg_user[k * n_c]
        for i in range(1, n_c):
            total = total + deg_user[k * n_c + i]
        totals.append(total)
    total_u = jnp.concatenate(totals, axis=1)
    inv_item = lax.rsqrt(jnp.maximum(total_i, 1).astype(F32))
    inv_user = lax.rsqrt(jnp.maximum(total_u, 1).astype(F32))
    user_scale[...] = jnp.transpose(jnp.broadcast_to(inv_user, (128, cu)))

    def scale_rows(i):
        rs = aligned(i * 32, 32, 32)
        by_user = user_scale[rs, :]
        for j in range(ni // 128):
            js = slice(j * 128, (j + 1) * 128)
            adj[rs, js] = ((by_user * mask_bf[rs, js].astype(F32)) * inv_item[:, js]).astype(BF16)

    arrived(mask_bf.at[own_users], S_SWAP)
    each(0, cu // 32, scale_rows)

    own_items = aligned(chip * piece, piece, 128)
    own_rows, own_lanes = aligned(emb * 8, 8, 8), aligned(col * lanes, lanes, 128)

    def step_u(k, items):
        pairs = n_c // 2
        mate = lax.rem(col, 2)
        for (p_o,) in far_first(pairs):
            p_to = lax.rem(lax.div(col, 2) + p_o, pairs)
            both = aligned(p_to * 2 * lanes, 2 * lanes, 128)
            part_u[k, :, both] = lane_dot(items, adj[both, :])
            for c_o in (1, 0):
                c_to = p_to * 2 + lax.rem(mate + c_o, 2)
                for (e_o,) in far_first(n_e):
                    tile = part_u.at[k, aligned(e_at[e_o] * 8, 8, 8), aligned(c_to * lanes, lanes, 128)]
                    if p_o or c_o or e_o:
                        remote(tile, recv_u.at[k, plane], S_RU + k, e_at[e_o], c_to, row).start()
                    else:
                        recv_u[k, plane] = tile[...]

    def step_i(k, users):
        for (x_o,) in far_first(n_x):
            there = aligned(x_at[x_o] * piece, piece, 128)
            part = jnp.dot(users, adj[:, there], preferred_element_type=F32)
            if x_o:
                part_i[k, :, there] = part
                remote(part_i.at[k, :, there], recv_i.at[k, chip], S_RI + k, emb, col, x_at[x_o] * 2 + core).start()
            else:
                recv_i[k, chip] = part

    def sum_u(k):
        arrived(recv_u.at[k, 0:n_p - 1], S_RU + k)
        total = recv_u[k, 0]
        for i in range(1, n_p):
            total = total + recv_u[k, i]
        return total.astype(BF16)

    def sum_i(k):
        arrived(recv_i.at[k, 0:n_x - 1], S_RI + k)
        total = recv_i[k, 0]
        for i in range(1, n_x):
            total = total + recv_i[k, i]
        return total.astype(BF16)

    def share_u(buf, k):
        for c_o, e_o in others(n_c, n_e):
            remote(buf.at[plane], buf.at[plane], S_GU + k, e_at[e_o], c_at[c_o], row).start()

    def share_i(buf, k):
        for (x_o,) in others(n_x):
            remote(buf.at[:, own_items], buf.at[:, own_items], S_GI + k, emb, col, x_at[x_o] * 2 + core).start()

    def whole_u(buf, k):
        arrived(buf.at[0:n_p - 1], S_GU + k)
        return jnp.concatenate(
            [jnp.concatenate([buf[c * n_e + e].astype(F32) for c in range(n_c)], axis=1) for e in range(n_e)],
            axis=0).astype(BF16)

    def whole_i(buf, k):
        arrived(buf.at[:, 0:piece * (n_x - 1)], S_GI + k)
        return buf[...]

    either(arrived, mine, user0_in.at[0:n_p - 1], user0_in, S_USER0)
    low = lax.broadcasted_iota(I32, (8, lanes), 1) < lanes // 2
    for t in range(n_c):
        for i in range(half):
            one = user0_in[2 * t * half + i].astype(F32)
            two = user0_in[(2 * t + 1) * half + i].astype(F32)
            ts = slice(t * lanes, (t + 1) * lanes)
            user0[i * cols:i * cols + 8, ts] = jnp.where(low, one, pltpu.roll(two, lanes // 2, 1))
            user0[i * cols + 8:i * cols + 16, ts] = jnp.where(low, pltpu.roll(one, lanes // 2, 1), two)
    step_i(0, user0[...].astype(BF16))
    n_in = n_r * half
    either(arrived, mine, recv_d.at[0:n_in - 1], recv_d.at[0:n_in], S_ITEM0)
    step_u(0, item0[...])

    def one_hot(ids, size):
        return (lax.broadcasted_iota(I32, (size, ids.shape[1]), 0) == lax.rem(ids, size)).astype(F32).astype(BF16)

    def hot_items(i):
        at = aligned(i * CHUNK, CHUNK, 128)
        for j in range(2):
            hot_item[j, :, at] = one_hot(trip[j + 1:j + 2, at], LOW)

    each(0, trip.shape[1] // CHUNK, hot_items)

    got = sum_i(0)
    item1[:, own_items] = got
    share_i(item1, 0)
    item_acc = item0[:, own_items].astype(F32) + got.astype(F32)
    got = sum_u(0)
    user1[plane] = got
    share_u(user1, 0)
    user_acc = user0[own_rows, own_lanes] + got.astype(F32)

    step_u(1, whole_i(item1, 0))
    step_i(1, whole_u(user1, 0))
    got = sum_u(1)
    user2[plane] = got
    share_u(user2, 1)
    user_acc = user_acc + got.astype(F32)
    got = sum_i(1)
    item2[:, own_items] = got
    share_i(item2, 1)
    item_acc = item_acc + got.astype(F32)

    step_i(2, whole_u(user2, 1))
    step_u(2, whole_i(item2, 1))

    item_acc = item_acc + sum_i(2).astype(F32)
    fin_item[...] = (item_acc / (NUM_LAYERS + 1)).astype(BF16)
    back = aligned(emb * sub, sub, 128)

    def own_send(e_o, k_o):
        e_to = lax.rem(in_half + e_o, half)
        remote(fin_item.at[aligned(e_to * cols, cols, 16), aligned(k_at[k_o] * sub, sub, 128)], item_own.at[:, back],
               S_OWN, half * core + e_to, col, chip * 2 + k_at[k_o]).start()

    for e_o, k_o in others(half, 2):
        own_send(e_o, k_o)

    @pl.when(jnp.logical_not(mine))
    def _():
        own_send(0, 0)

    @pl.when(mine)
    def _():
        item_own[:, back] = fin_item[here_rows, aligned(core * sub, sub, 128)]

    user_acc = user_acc + sum_u(2).astype(F32)
    fin_tile[0] = (user_acc / (NUM_LAYERS + 1)).astype(BF16)
    e_fin = half * core + lax.div(emb, 2)
    slot = lax.rem(emb, 2) * (n_x * n_c) + chip * n_c + col
    fin_mine = e_fin == emb

    def fin_send(x_o, c_o, k_o):
        remote(fin_tile.at[0], fin_all.at[slot], S_FIN, e_fin, c_at[c_o], x_at[x_o] * 2 + k_at[k_o]).start()

    for offsets in others(n_x, n_c, 2):
        fin_send(*offsets)

    @pl.when(jnp.logical_not(fin_mine))
    def _():
        fin_send(0, 0, 0)

    @pl.when(fin_mine)
    def _():
        fin_all[slot] = fin_tile[0]

    either(arrived, mine, item_own.at[:, 0:sub * (n_e - 1)], item_own, S_OWN)
    out_item[...] = item_own[...]

    n_hi = width // LOW
    by_hi = jnp.concatenate([item_own[:, j * LOW:(j + 1) * LOW] for j in range(n_hi)], axis=0)
    hi_base = (col * n_r + row) * n_hi

    def pick(hot, high, table, count):
        found = jnp.dot(table, hot, preferred_element_type=F32)
        total = jnp.zeros((cols, high.shape[1]), F32)
        for j in range(count):
            total = total + jnp.where(high == j, found[j * cols:(j + 1) * cols], 0.0)
        return total

    def pick_side(i, at):
        return pick(hot_item[i - 1, :, at], lax.div(trip[i:i + 1, at], LOW) - hi_base, by_hi, n_hi)

    n_chunk, per_chunk = trip.shape[1] // CHUNK, CHUNK // 128

    def d_send(q):
        @pl.when(q != block)
        def _():
            remote(part_d.at[:, aligned(q * 128, 128, 128)], recv_d.at[block], S_D,
                   emb, lax.rem(q, n_c), lax.div(q, n_c)).start()

    def pick_items(i):
        chunk = lax.rem(lax.div(block, per_chunk) + i, n_chunk)
        at = aligned(chunk * CHUNK, CHUNK, 128)
        part_d[:, at] = pick_side(1, at) - pick_side(2, at)
        for j in range(per_chunk):
            d_send(chunk * per_chunk + j)

    each(1, n_chunk + 1, pick_items)
    recv_d[block] = part_d[:, aligned(block * 128, 128, 128)]

    left(mask_bf.at[own_users], S_SWAP)
    either(left, mine, recv_d.at[0:n_in - 1], recv_d.at[0:n_in], S_ITEM0)
    either(left, mine, user0_in.at[0:n_p - 1], user0_in, S_USER0)
    left(deg_item.at[0:n_r - 1], S_DI)
    left(deg_user.at[0:2 * n_c - 1], S_DU)
    for k in range(3):
        left(recv_u.at[k, 0:n_p - 1], S_RU + k)
        left(recv_i.at[k, 0:n_x - 1], S_RI + k)
    left(user1.at[0:n_p - 1], S_GU)
    left(user2.at[0:n_p - 1], S_GU + 1)
    left(item1.at[:, 0:piece * (n_x - 1)], S_GI)
    left(item2.at[:, 0:piece * (n_x - 1)], S_GI + 1)
    either(left, mine, item_own.at[:, 0:sub * (n_e - 1)], item_own, S_OWN)

    either(arrived, fin_mine, fin_all.at[0:n_b - 1], fin_all, S_FIN)
    n_t = n_x * n_c
    here = chip * n_c + lax.div(core * n_c + col, 2)
    wide = jnp.concatenate([fin_all[here], fin_all[n_t + here]], axis=0).astype(F32)
    wide = jnp.where(lax.rem(col, 2) == 1, pltpu.roll(wide, lanes // 2, 1), wide)
    out_user[...] = wide[:, :lanes // 2].astype(BF16)
    by_tile = jnp.concatenate(
        [fin_all[s * n_t + t].astype(F32) for t in range(n_t) for s in range(2)], axis=0).astype(BF16)
    ids = trip[0:1, aligned(block * 128, 128, 128)]
    e_user = pick(one_hot(ids, 128), lax.div(ids, 128), by_tile, n_t)

    arrived(recv_d.at[0:n_b - 1], S_D)
    diff = recv_d[0]
    for i in range(1, n_b):
        diff = diff + recv_d[i]
    zpart[emb] = jnp.sum(e_user * diff, axis=0, keepdims=True)
    for (e_o,) in others(n_e):
        remote(zpart.at[emb], zpart.at[emb], S_Z, e_at[e_o], col, row).start()
    either(left, fin_mine, fin_all.at[0:n_b - 1], fin_all, S_FIN)
    left(recv_d.at[0:n_b - 1], S_D)
    arrived(zpart.at[0:n_e - 1], S_Z)
    score = zpart[0]
    for i in range(1, n_e):
        score = score + zpart[i]
    scores[block] = score
    for x_o, c_o, k_o in others(n_x, n_c, 2):
        remote(scores.at[block], scores.at[block], S_S, emb, c_at[c_o], x_at[x_o] * 2 + k_at[k_o]).start()
    left(zpart.at[0:n_e - 1], S_Z)
    arrived(scores.at[0:n_b - 1], S_S)
    for i in range(n_b):
        score_out[i:i + 1, :] = scores[i]
    left(scores.at[0:n_b - 1], S_S)


def solution(mesh):
    dims = n_e, n_c, n_r = mesh.shape["emb"], mesh.shape["col"], mesh.shape["row"]

    def local_fn(mask_blk, user_sh, item_sh, triples):
        rows_u = mask_blk.shape[0]
        width, cols = item_sh.shape
        num_trip = triples.shape[0]
        n_x, n_p, n_b, half = n_r // 2, n_c * n_e, n_r * n_c, n_e // 2
        sub = width // n_e
        ni, cu, kd = n_r * sub, 2 * rows_u, half * cols
        piece, lanes = ni // n_x, cu // n_c
        dma = pltpu.SemaphoreType.DMA
        vmem, hbm = pl.BlockSpec(memory_space=pltpu.VMEM), pl.BlockSpec(memory_space=pltpu.HBM)
        scratch = [
            pltpu.VMEM((cols, user_sh.shape[0]), BF16),
            pltpu.VMEM((8, lanes), BF16),
            pltpu.VMEM((cols, lanes), F32),
            pltpu.VMEM((cols, width), BF16),
            pltpu.VMEM((3, num_trip), I32),
            pltpu.VMEM((n_r, rows_u, width), I32),
            pltpu.VMEM((rows_u, 128), I32),
            pltpu.VMEM((cu, ni), BF16),
            pltpu.VMEM((cu, ni), BF16),
            pltpu.VMEM((n_r, 1, ni), I32),
            pltpu.VMEM((2 * n_c, 1, rows_u), I32),
            pltpu.VMEM((cu, 128), F32),
            pltpu.VMEM((2 * n_c * half, 8, lanes), BF16),
            pltpu.VMEM((kd, cu), F32),
            pltpu.VMEM((kd, ni), BF16),
            pltpu.VMEM((kd, ni), BF16),
            pltpu.VMEM((kd, ni), BF16),
            pltpu.VMEM((n_p, 8, lanes), BF16),
            pltpu.VMEM((n_p, 8, lanes), BF16),
            pltpu.VMEM((3, kd, cu), F32),
            pltpu.VMEM((3, n_p, 8, lanes), F32),
            pltpu.VMEM((3, kd, ni), F32),
            pltpu.VMEM((3, n_x, kd, piece), F32),
            pltpu.VMEM((1, 8, lanes), BF16),
            pltpu.VMEM((kd, piece), BF16),
            pltpu.VMEM((cols, width), BF16),
            pltpu.VMEM((2 * n_x * n_c, 8, lanes), BF16),
            pltpu.VMEM((2, LOW, num_trip), BF16),
            pltpu.VMEM((cols, num_trip), F32),
            pltpu.VMEM((n_b, cols, 128), F32),
            pltpu.VMEM((n_e, 1, 128), F32),
            pltpu.VMEM((n_b, 1, 128), F32),
            dma((n_r,)), dma((3,)), dma((NUM_SEMS,)), dma((NUM_SEMS,)),
        ]
        user_t, item_t, score = pl.pallas_call(
            functools.partial(kernel, dims),
            out_shape=(jax.ShapeDtypeStruct((cols, user_sh.shape[0]), BF16),
                       jax.ShapeDtypeStruct((cols, width), BF16),
                       jax.ShapeDtypeStruct((n_b, 128), F32)),
            in_specs=[hbm, hbm, hbm, hbm],
            out_specs=(vmem, vmem, vmem),
            scratch_shapes=scratch,
            compiler_params=pltpu.CompilerParams(collective_id=0, has_side_effects=True, vmem_limit_bytes=40 << 20),
        )(mask_blk, *(pltpu.with_memory_space_constraint(v.T, pltpu.HBM) for v in (user_sh, item_sh, triples)))
        return user_t.T, item_t.T, jax.nn.softplus(-score.reshape(num_trip))

    return jax.shard_map(
        local_fn, mesh=mesh,
        in_specs=(P("row", "col"), P(("row", "col"), "emb"), P(("col", "row"), "emb"), P()),
        out_specs=(P(("row", "col"), "emb"), P(("col", "row"), "emb"), P()),
        check_vma=False)
```

time: 89.7 us -> 80.2 us (0.89)
  Pallas kernels: 84.7 us -> 77.6 us
  local copies, waits for them, and re-layouts: 3.58 us -> 1.22 us
    pallas_call x1, Pallas kernels: 84.7 us -> 77.6 us  [local_fn(): pl.pallas_call(functools.partial(kernel, dims), out_shape=(jax.ShapeDtype...]
    unnamed x8 -> x2, local copies, waits for them, and re-layouts: 3.58 us -> 1.22 us
where the time goes in v3:
time: 80.2 us; the launch traced here: 80.1 us
  Pallas kernels  77.6 us (97%)
  local copies, waits for them, and re-layouts  1.22 us (2%)
    pallas_call x1, Pallas kernels, local_fn(): pl.pallas_call(functools.partial(kernel, dims), out_shape=(jax.ShapeDtype...  77.6 us

profile of v3, /device:TPU:1, one launch (start us, length us, event | category | flops | bytes accessed | tf_op | source)
XLA Modules:
  0.0 80.1 jit_solution(4178775003464178207)
XLA Ops:
  0.6 77.6 %shard_map.67 = (bf16[16,64]{1,0:T(8,128)(2,1)S(1)}, bf16[16,2048]{1,0:T(8,128)(2,1)S(1)}, f32[32,128]{1,0:T(8,128)S(1)}) custom-call(s32[256,16384]{1,0:T(8,128)} %mask_hbm.1, bf16[16,64]{1,0:T(8,128)(2,1)} %bitcast.25, bf16[16,2048]{1,0:T(8,128)(2,1)} %bitcast.23, s32[3,4096]{1,0:T(4,128)} %bitcast.24), custom_call_target="tpu_custom_call" | custom-call | tf_op jit(solution)/shard_map/pallas_call | solution.py:489
  78.3 0.6 compare_select_fusion
  78.9 0.6 copy.9
  79.5 0.6 copy.10

commit v4 on v3

--- a/solution.py
+++ b/solution.py
@@ -11,6 +11,7 @@
 F32, BF16, I32 = jnp.float32, jnp.bfloat16, jnp.int32
 NUM_LAYERS = 3
 CHUNK = 512
+PICK = 1024
 LOW = 256
 
 
@@ -49,11 +50,11 @@
 
 
 def kernel(dims, mask_hbm, user_hbm, item_hbm, trip_hbm, out_user, out_item, score_out,
-           user_in, user_pack, user_wide, item_in, trip, mask_raw, row_acc, mask_bf, adj, deg_item, deg_user, user_scale,
+           user_in, user_pack, user_wide, item_in, trip, mask_part, mask_raw, row_acc, mask_bf, adj, deg_item, deg_user, user_scale,
            user0_in, user0, item0, item1, item2,
            user1, user2, part_u, recv_u, part_i, recv_i,
            fin_tile, fin_item, item_own, fin_all, hot_item, part_d, recv_d, zpart, scores,
-           sem_raw, sem_in, sem_send, sem_recv):
+           sem_part, sem_raw, sem_in, sem_send, sem_recv):
     n_e, n_c, n_r = dims
     n_x, half = n_r // 2, n_e // 2
     n_p = n_c * n_e
@@ -98,6 +99,10 @@
         def _():
             wait(full, stage)
 
+    def part(i):
+        return pltpu.make_async_copy(
+            mask_hbm.at[:, aligned(i * width + emb * sub, sub, 128)], mask_part.at[i], sem_part.at[i])
+
     def raw(i):
         return pltpu.make_async_copy(
             mask_hbm.at[:, i * width:(i + 1) * width], mask_raw.at[i], sem_raw.at[i])
@@ -115,29 +120,19 @@
     for c_o, e_o, k_o in far_first(n_c, n_e, 2):
         if c_o:
             hello(e_at[e_o], c_at[c_o], chip * 2 + k_at[k_o])
+    for copy in fetch:
+        copy.start()
+    for i in range(n_r):
+        part(i).start()
     for i in range(n_r):
         raw(i).start()
-    for copy in fetch:
-        copy.start()
 
     own_users = aligned(core * rows_u, rows_u, 128)
-    at_emb = aligned(emb * sub, sub, 128)
     for i in range(n_r):
-        raw(i).wait()
-        mask_bf[own_users, i * sub:(i + 1) * sub] = mask_raw[i, :, at_emb].astype(F32).astype(BF16)
-
-        def row_sums(t):
-            rs = aligned(t * 32, 32, 32)
-            total = mask_raw[i, rs, 0:128]
-            for j in range(1, width // 128):
-                total = total + mask_raw[i, rs, j * 128:(j + 1) * 128]
-            row_acc[rs, :] = total if i == 0 else row_acc[rs, :] + total
-
-        each(0, rows_u // 32, row_sums)
-    own_mask = mask_bf[own_users, :]
-    deg_item[row] = jnp.dot(jnp.ones((8, rows_u), BF16), own_mask, preferred_element_type=F32)[0:1].astype(I32)
-    own_part = core * n_c + col
-    deg_user[own_part] = jnp.sum(jnp.transpose(row_acc[...].astype(F32)), axis=0, keepdims=True).astype(I32)
+        part(i).wait()
+        mask_bf[own_users, i * sub:(i + 1) * sub] = mask_part[i].astype(F32).astype(BF16)
+    deg_item[row] = jnp.dot(
+        jnp.ones((8, rows_u), BF16), mask_bf[own_users, :], preferred_element_type=F32)[0:1].astype(I32)
 
     fetch[0].wait()
     user_wide[...] = jnp.zeros_like(user_wide)
@@ -148,8 +143,6 @@
     fetch[2].wait()
     pl.semaphore_wait(barrier, n_r * n_e - 1 + 2 * n_e * (n_c - 1))
 
-    for c_o, k_o in others(n_c, 2):
-        remote(deg_user.at[own_part], deg_user.at[own_part], S_DU, emb, c_at[c_o], chip * 2 + k_at[k_o]).start()
     for x_o, k_o in others(n_x, 2):
         remote(deg_item.at[row], deg_item.at[row], S_DI, emb, col, x_at[x_o] * 2 + k_at[k_o]).start()
 
@@ -180,6 +173,32 @@
     def _():
         item0[here_rows, here_items] = item_in[:, aligned(emb * sub, sub, 128)]
         user0_in[user_slot] = user_pack[...]
+
+    for i in range(n_r):
+        raw(i).wait()
+
+        def row_sums(t):
+            rs = aligned(t * 32, 32, 32)
+            total = mask_raw[i, rs, 0:128]
+            for j in range(1, width // 128):
+                total = total + mask_raw[i, rs, j * 128:(j + 1) * 128]
+            row_acc[rs, :] = total if i == 0 else row_acc[rs, :] + total
+
+        each(0, rows_u // 32, row_sums)
+    own_part = core * n_c + col
+    deg_user[own_part] = jnp.sum(jnp.transpose(row_acc[...].astype(F32)), axis=0, keepdims=True).astype(I32)
+    for c_o, k_o in others(n_c, 2):
+        remote(deg_user.at[own_part], deg_user.at[own_part], S_DU, emb, c_at[c_o], chip * 2 + k_at[k_o]).start()
+
+    def one_hot(ids, size):
+        return (lax.broadcasted_iota(I32, (size, ids.shape[1]), 0) == lax.rem(ids, size)).astype(F32).astype(BF16)
+
+    def hot_items(i):
+        at = aligned(i * CHUNK, CHUNK, 128)
+        for j in range(2):
+            hot_item[j, :, at] = one_hot(trip[j + 1:j + 2, at], LOW)
+
+    each(0, trip.shape[1] // CHUNK, hot_items)
 
     arrived(deg_item.at[0:n_r - 1], S_DI)
     arrived(deg_user.at[0:2 * n_c - 1], S_DU)
@@ -282,16 +301,6 @@
     either(arrived, mine, recv_d.at[0:n_in - 1], recv_d.at[0:n_in], S_ITEM0)
     step_u(0, item0[...])
 
-    def one_hot(ids, size):
-        return (lax.broadcasted_iota(I32, (size, ids.shape[1]), 0) == lax.rem(ids, size)).astype(F32).astype(BF16)
-
-    def hot_items(i):
-        at = aligned(i * CHUNK, CHUNK, 128)
-        for j in range(2):
-            hot_item[j, :, at] = one_hot(trip[j + 1:j + 2, at], LOW)
-
-    each(0, trip.shape[1] // CHUNK, hot_items)
-
     got = sum_i(0)
     item1[:, own_items] = got
     share_i(item1, 0)
@@ -372,7 +381,7 @@
     def pick_side(i, at):
         return pick(hot_item[i - 1, :, at], lax.div(trip[i:i + 1, at], LOW) - hi_base, by_hi, n_hi)
 
-    n_chunk, per_chunk = trip.shape[1] // CHUNK, CHUNK // 128
+    n_chunk, per_chunk = trip.shape[1] // PICK, PICK // 128
 
     def d_send(q):
         @pl.when(q != block)
@@ -382,7 +391,7 @@
 
     def pick_items(i):
         chunk = lax.rem(lax.div(block, per_chunk) + i, n_chunk)
-        at = aligned(chunk * CHUNK, CHUNK, 128)
+        at = aligned(chunk * PICK, PICK, 128)
         part_d[:, at] = pick_side(1, at) - pick_side(2, at)
         for j in range(per_chunk):
             d_send(chunk * per_chunk + j)
@@ -438,6 +447,12 @@
     left(scores.at[0:n_b - 1], S_S)
 
 
+def finish(user_in, item_in, score_in, out_user, out_item, loss):
+    out_user[...] = user_in[...]
+    out_item[...] = item_in[...]
+    loss[...] = jax.nn.softplus(-score_in[...])
+
+
 def solution(mesh):
     dims = n_e, n_c, n_r = mesh.shape["emb"], mesh.shape["col"], mesh.shape["row"]
 
@@ -457,6 +472,7 @@
             pltpu.VMEM((cols, lanes), F32),
             pltpu.VMEM((cols, width), BF16),
             pltpu.VMEM((3, num_trip), I32),
+            pltpu.VMEM((n_r, rows_u, sub), I32),
             pltpu.VMEM((n_r, rows_u, width), I32),
             pltpu.VMEM((rows_u, 128), I32),
             pltpu.VMEM((cu, ni), BF16),
@@ -484,7 +500,7 @@
             pltpu.VMEM((n_b, cols, 128), F32),
             pltpu.VMEM((n_e, 1, 128), F32),
             pltpu.VMEM((n_b, 1, 128), F32),
-            dma((n_r,)), dma((3,)), dma((NUM_SEMS,)), dma((NUM_SEMS,)),
+            dma((n_r,)), dma((n_r,)), dma((3,)), dma((NUM_SEMS,)), dma((NUM_SEMS,)),
         ]
         user_t, item_t, score = pl.pallas_call(
             functools.partial(kernel, dims),
@@ -496,7 +512,14 @@
             scratch_shapes=scratch,
             compiler_params=pltpu.CompilerParams(collective_id=0, has_side_effects=True, vmem_limit_bytes=40 << 20),
         )(mask_blk, *(pltpu.with_memory_space_constraint(v.T, pltpu.HBM) for v in (user_sh, item_sh, triples)))
-        return user_t.T, item_t.T, jax.nn.softplus(-score.reshape(num_trip))
+        user_t, item_t, loss = pl.pallas_call(
+            finish,
+            out_shape=(jax.ShapeDtypeStruct(user_t.shape, BF16), jax.ShapeDtypeStruct(item_t.shape, BF16),
+                       jax.ShapeDtypeStruct(score.shape, F32)),
+            in_specs=[vmem] * 3,
+            compiler_params=pltpu.CompilerParams(vmem_limit_bytes=1 << 20),
+        )(user_t, item_t, score)
+        return user_t.T, item_t.T, loss.reshape(num_trip)
 
     return jax.shard_map(
         local_fn, mesh=mesh,

time: 80.2 us -> 79 us (0.985)
  local copies, waits for them, and re-layouts: 1.22 us -> 0 us
    unnamed x2 -> x0, local copies, waits for them, and re-layouts: 1.22 us -> none
where the time goes in v4:
time: 79 us; the launch traced here: 78.9 us
  Pallas kernels  78.2 us (99%)
    pallas_call x1, Pallas kernels, local_fn(): pl.pallas_call(functools.partial(kernel, dims), out_shape=(jax.ShapeDtype...  77.6 us

profile of v4, /device:TPU:1, one launch (start us, length us, event | category | flops | bytes accessed | tf_op | source)
XLA Modules:
  0.0 78.9 jit_solution(17371432558014718533)
XLA Ops:
  0.6 77.6 %shard_map.67 = (bf16[16,64]{1,0:T(8,128)(2,1)S(1)}, bf16[16,2048]{1,0:T(8,128)(2,1)S(1)}, f32[32,128]{1,0:T(8,128)S(1)}) custom-call(s32[256,16384]{1,0:T(8,128)} %mask_hbm.1, bf16[16,64]{1,0:T(8,128)(2,1)} %bitcast.8, bf16[16,2048]{1,0:T(8,128)(2,1)} %bitcast.6, s32[3,4096]{1,0:T(4,128)} %bitcast.7), custom_call_target="tpu_custom_call" | custom-call | tf_op jit(solution)/shard_map/pallas_call | solution.py:505
  78.2 0.6 shard_map.68

commit v5 on v4

--- a/solution.py
+++ b/solution.py
@@ -99,13 +99,16 @@
         def _():
             wait(full, stage)
 
+    odd = lax.rem(emb, 2)
+    n_half = n_r // 2
+
     def part(i):
         return pltpu.make_async_copy(
             mask_hbm.at[:, aligned(i * width + emb * sub, sub, 128)], mask_part.at[i], sem_part.at[i])
 
     def raw(i):
         return pltpu.make_async_copy(
-            mask_hbm.at[:, i * width:(i + 1) * width], mask_raw.at[i], sem_raw.at[i])
+            mask_hbm.at[:, aligned((odd * n_half + i) * width, width, 128)], mask_raw.at[i], sem_raw.at[i])
 
     fetch = [pltpu.make_async_copy(src, dst, sem_in.at[i]) for i, (src, dst) in enumerate(
         ((user_hbm, user_in), (item_hbm, item_in), (trip_hbm, trip)))]
@@ -124,13 +127,13 @@
         copy.start()
     for i in range(n_r):
         part(i).start()
-    for i in range(n_r):
-        raw(i).start()
 
     own_users = aligned(core * rows_u, rows_u, 128)
     for i in range(n_r):
         part(i).wait()
         mask_bf[own_users, i * sub:(i + 1) * sub] = mask_part[i].astype(F32).astype(BF16)
+    for i in range(n_half):
+        raw(i).start()
     deg_item[row] = jnp.dot(
         jnp.ones((8, rows_u), BF16), mask_bf[own_users, :], preferred_element_type=F32)[0:1].astype(I32)
 
@@ -174,7 +177,7 @@
         item0[here_rows, here_items] = item_in[:, aligned(emb * sub, sub, 128)]
         user0_in[user_slot] = user_pack[...]
 
-    for i in range(n_r):
+    for i in range(n_half):
         raw(i).wait()
 
         def row_sums(t):
@@ -185,10 +188,11 @@
             row_acc[rs, :] = total if i == 0 else row_acc[rs, :] + total
 
         each(0, rows_u // 32, row_sums)
-    own_part = core * n_c + col
+    own_part = (core * n_c + col) * 2 + odd
+    e_pair = [emb, emb + 1 - 2 * odd]
     deg_user[own_part] = jnp.sum(jnp.transpose(row_acc[...].astype(F32)), axis=0, keepdims=True).astype(I32)
-    for c_o, k_o in others(n_c, 2):
-        remote(deg_user.at[own_part], deg_user.at[own_part], S_DU, emb, c_at[c_o], chip * 2 + k_at[k_o]).start()
+    for c_o, k_o, e_o in others(n_c, 2, 2):
+        remote(deg_user.at[own_part], deg_user.at[own_part], S_DU, e_pair[e_o], c_at[c_o], chip * 2 + k_at[k_o]).start()
 
     def one_hot(ids, size):
         return (lax.broadcasted_iota(I32, (size, ids.shape[1]), 0) == lax.rem(ids, size)).astype(F32).astype(BF16)
@@ -201,15 +205,15 @@
     each(0, trip.shape[1] // CHUNK, hot_items)
 
     arrived(deg_item.at[0:n_r - 1], S_DI)
-    arrived(deg_user.at[0:2 * n_c - 1], S_DU)
+    arrived(deg_user.at[0:4 * n_c - 1], S_DU)
     total_i = deg_item[0]
     for i in range(1, n_r):
         total_i = total_i + deg_item[i]
     totals = []
     for k in range(2):
-        total = deg_user[k * n_c]
-        for i in range(1, n_c):
-            total = total + deg_user[k * n_c + i]
+        total = deg_user[k * 2 * n_c]
+        for i in range(1, 2 * n_c):
+            total = total + deg_user[k * 2 * n_c + i]
         totals.append(total)
     total_u = jnp.concatenate(totals, axis=1)
     inv_item = lax.rsqrt(jnp.maximum(total_i, 1).astype(F32))
@@ -396,14 +400,15 @@
         for j in range(per_chunk):
             d_send(chunk * per_chunk + j)
 
-    each(1, n_chunk + 1, pick_items)
+    for (i,) in far_first(n_chunk):
+        pick_items(i)
     recv_d[block] = part_d[:, aligned(block * 128, 128, 128)]
 
     left(mask_bf.at[own_users], S_SWAP)
     either(left, mine, recv_d.at[0:n_in - 1], recv_d.at[0:n_in], S_ITEM0)
     either(left, mine, user0_in.at[0:n_p - 1], user0_in, S_USER0)
     left(deg_item.at[0:n_r - 1], S_DI)
-    left(deg_user.at[0:2 * n_c - 1], S_DU)
+    left(deg_user.at[0:4 * n_c - 1], S_DU)
     for k in range(3):
         left(recv_u.at[k, 0:n_p - 1], S_RU + k)
         left(recv_i.at[k, 0:n_x - 1], S_RI + k)
@@ -473,12 +478,12 @@
             pltpu.VMEM((cols, width), BF16),
             pltpu.VMEM((3, num_trip), I32),
             pltpu.VMEM((n_r, rows_u, sub), I32),
-            pltpu.VMEM((n_r, rows_u, width), I32),
+            pltpu.VMEM((n_x, rows_u, width), I32),
             pltpu.VMEM((rows_u, 128), I32),
             pltpu.VMEM((cu, ni), BF16),
             pltpu.VMEM((cu, ni), BF16),
             pltpu.VMEM((n_r, 1, ni), I32),
-            pltpu.VMEM((2 * n_c, 1, rows_u), I32),
+            pltpu.VMEM((4 * n_c, 1, rows_u), I32),
             pltpu.VMEM((cu, 128), F32),
             pltpu.VMEM((2 * n_c * half, 8, lanes), BF16),
             pltpu.VMEM((kd, cu), F32),

time: 79 us -> 78.6 us (level)
  no operation moved by 1% of the time
where the time goes in v5:
time: 78.6 us; the launch traced here: 78.5 us
  Pallas kernels  77.8 us (99%)
    pallas_call x1, Pallas kernels, local_fn(): pl.pallas_call(functools.partial(kernel, dims), out_shape=(jax.ShapeDtype...  77.2 us

profile of v5, /device:TPU:1, one launch (start us, length us, event | category | flops | bytes accessed | tf_op | source)
XLA Modules:
  0.0 78.5 jit_solution(15723348839839543489)
XLA Ops:
  0.6 77.2 %shard_map.67 = (bf16[16,64]{1,0:T(8,128)(2,1)S(1)}, bf16[16,2048]{1,0:T(8,128)(2,1)S(1)}, f32[32,128]{1,0:T(8,128)S(1)}) custom-call(s32[256,16384]{1,0:T(8,128)} %mask_hbm.1, bf16[16,64]{1,0:T(8,128)(2,1)} %bitcast.8, bf16[16,2048]{1,0:T(8,128)(2,1)} %bitcast.6, s32[3,4096]{1,0:T(4,128)} %bitcast.7), custom_call_target="tpu_custom_call" | custom-call | tf_op jit(solution)/shard_map/pallas_call | solution.py:510
  77.8 0.6 shard_map.68

commit v6 on v4

--- a/solution.py
+++ b/solution.py
@@ -124,13 +124,13 @@
         copy.start()
     for i in range(n_r):
         part(i).start()
-    for i in range(n_r):
-        raw(i).start()
 
     own_users = aligned(core * rows_u, rows_u, 128)
     for i in range(n_r):
         part(i).wait()
         mask_bf[own_users, i * sub:(i + 1) * sub] = mask_part[i].astype(F32).astype(BF16)
+    for i in range(n_r):
+        raw(i).start()
     deg_item[row] = jnp.dot(
         jnp.ones((8, rows_u), BF16), mask_bf[own_users, :], preferred_element_type=F32)[0:1].astype(I32)
 
@@ -396,7 +396,8 @@
         for j in range(per_chunk):
             d_send(chunk * per_chunk + j)
 
-    each(1, n_chunk + 1, pick_items)
+    for (i,) in far_first(n_chunk):
+        pick_items(i)
     recv_d[block] = part_d[:, aligned(block * 128, 128, 128)]
 
     left(mask_bf.at[own_users], S_SWAP)

time: 79 us -> 76.8 us (0.972)
  Pallas kernels: 78.2 us -> 76 us
    pallas_call x1, Pallas kernels: 77.6 us -> 75.4 us  [local_fn(): pl.pallas_call(functools.partial(kernel, dims), out_shape=(jax.ShapeDtype...]
where the time goes in v6:
time: 76.8 us; the launch traced here: 76.7 us
  Pallas kernels  76 us (99%)
    pallas_call x1, Pallas kernels, local_fn(): pl.pallas_call(functools.partial(kernel, dims), out_shape=(jax.ShapeDtype...  75.4 us

profile of v6, /device:TPU:1, one launch (start us, length us, event | category | flops | bytes accessed | tf_op | source)
XLA Modules:
  0.0 76.7 jit_solution(8837821557634969728)
XLA Ops:
  0.6 75.4 %shard_map.67 = (bf16[16,64]{1,0:T(8,128)(2,1)S(1)}, bf16[16,2048]{1,0:T(8,128)(2,1)S(1)}, f32[32,128]{1,0:T(8,128)S(1)}) custom-call(s32[256,16384]{1,0:T(8,128)} %mask_hbm.1, bf16[16,64]{1,0:T(8,128)(2,1)} %bitcast.8, bf16[16,2048]{1,0:T(8,128)(2,1)} %bitcast.6, s32[3,4096]{1,0:T(4,128)} %bitcast.7), custom_call_target="tpu_custom_call" | custom-call | tf_op jit(solution)/shard_map/pallas_call | solution.py:506
  76.0 0.6 shard_map.68

commit v7 on v6

--- a/solution.py
+++ b/solution.py
@@ -110,6 +110,11 @@
     fetch = [pltpu.make_async_copy(src, dst, sem_in.at[i]) for i, (src, dst) in enumerate(
         ((user_hbm, user_in), (item_hbm, item_in), (trip_hbm, trip)))]
 
+    for copy in fetch:
+        copy.start()
+    for i in range(n_r):
+        part(i).start()
+
     barrier = pltpu.get_barrier_semaphore()
 
     def hello(e, c, r):
@@ -120,19 +125,12 @@
     for c_o, e_o, k_o in far_first(n_c, n_e, 2):
         if c_o:
             hello(e_at[e_o], c_at[c_o], chip * 2 + k_at[k_o])
-    for copy in fetch:
-        copy.start()
-    for i in range(n_r):
-        part(i).start()
 
     own_users = aligned(core * rows_u, rows_u, 128)
     for i in range(n_r):
         part(i).wait()
-        mask_bf[own_users, i * sub:(i + 1) * sub] = mask_part[i].astype(F32).astype(BF16)
     for i in range(n_r):
         raw(i).start()
-    deg_item[row] = jnp.dot(
-        jnp.ones((8, rows_u), BF16), mask_bf[own_users, :], preferred_element_type=F32)[0:1].astype(I32)
 
     fetch[0].wait()
     user_wide[...] = jnp.zeros_like(user_wide)
@@ -143,9 +141,6 @@
     fetch[2].wait()
     pl.semaphore_wait(barrier, n_r * n_e - 1 + 2 * n_e * (n_c - 1))
 
-    for x_o, k_o in others(n_x, 2):
-        remote(deg_item.at[row], deg_item.at[row], S_DI, emb, col, x_at[x_o] * 2 + k_at[k_o]).start()
-
     here_rows = aligned(in_half * cols, cols, 16)
     here_items = aligned(row * sub, sub, 128)
     user_slot = (core * n_c + col) * half + in_half
@@ -155,8 +150,6 @@
 
     for c_o, e_o in others(n_c, n_e):
         user0_send(c_o, e_o)
-    remote(mask_bf.at[own_users], mask_bf.at[own_users], S_SWAP, emb, col, chip * 2 + 1 - core).start()
-
     def item0_send(x_o, e_o):
         remote(item_in.at[:, aligned(e_at[e_o] * sub, sub, 128)], item0.at[here_rows, here_items], S_ITEM0,
                e_at[e_o], col, x_at[x_o] * 2 + home).start()
@@ -173,6 +166,16 @@
     def _():
         item0[here_rows, here_items] = item_in[:, aligned(emb * sub, sub, 128)]
         user0_in[user_slot] = user_pack[...]
+
+    for i in range(n_r):
+        mask_bf[own_users, i * sub:(i + 1) * sub] = mask_part[i].astype(F32).astype(BF16)
+    deg_item[row] = jnp.dot(
+        jnp.ones((8, rows_u), BF16), mask_bf[own_users, :], preferred_element_type=F32)[0:1].astype(I32)
+
+    for x_o, k_o in others(n_x, 2):
+        remote(deg_item.at[row], deg_item.at[row], S_DI, emb, col, x_at[x_o] * 2 + k_at[k_o]).start()
+
+    remote(mask_bf.at[own_users], mask_bf.at[own_users], S_SWAP, emb, col, chip * 2 + 1 - core).start()
 
     for i in range(n_r):
         raw(i).wait()
@@ -246,7 +249,7 @@
                         recv_u[k, plane] = tile[...]
 
     def step_i(k, users):
-        for (x_o,) in far_first(n_x):
+        for (x_o,) in (*others(n_x), (0,)):
             there = aligned(x_at[x_o] * piece, piece, 128)
             part = jnp.dot(users, adj[:, there], preferred_element_type=F32)
             if x_o:

time: 76.8 us -> 75.8 us (0.987)
  Pallas kernels: 76 us -> 75 us
    pallas_call x1, Pallas kernels: 75.4 us -> 74.4 us  [local_fn(): pl.pallas_call(functools.partial(kernel, dims), out_shape=(jax.ShapeDtype...]
where the time goes in v7:
time: 75.8 us; the launch traced here: 75.7 us
  Pallas kernels  75 us (99%)
    pallas_call x1, Pallas kernels, local_fn(): pl.pallas_call(functools.partial(kernel, dims), out_shape=(jax.ShapeDtype...  74.4 us

profile of v7, /device:TPU:1, one launch (start us, length us, event | category | flops | bytes accessed | tf_op | source)
XLA Modules:
  0.0 75.7 jit_solution(11468390568059733972)
XLA Ops:
  0.6 74.4 %shard_map.67 = (bf16[16,64]{1,0:T(8,128)(2,1)S(1)}, bf16[16,2048]{1,0:T(8,128)(2,1)S(1)}, f32[32,128]{1,0:T(8,128)S(1)}) custom-call(s32[256,16384]{1,0:T(8,128)} %mask_hbm.1, bf16[16,64]{1,0:T(8,128)(2,1)} %bitcast.8, bf16[16,2048]{1,0:T(8,128)(2,1)} %bitcast.6, s32[3,4096]{1,0:T(4,128)} %bitcast.7), custom_call_target="tpu_custom_call" | custom-call | tf_op jit(solution)/shard_map/pallas_call | solution.py:509
  75.0 0.6 shard_map.68

commit v8 on v7

--- a/solution.py
+++ b/solution.py
@@ -181,13 +181,13 @@
         raw(i).wait()
 
         def row_sums(t):
-            rs = aligned(t * 32, 32, 32)
+            rs = aligned(t * 64, 64, 64)
             total = mask_raw[i, rs, 0:128]
             for j in range(1, width // 128):
                 total = total + mask_raw[i, rs, j * 128:(j + 1) * 128]
             row_acc[rs, :] = total if i == 0 else row_acc[rs, :] + total
 
-        each(0, rows_u // 32, row_sums)
+        each(0, rows_u // 64, row_sums)
     own_part = core * n_c + col
     deg_user[own_part] = jnp.sum(jnp.transpose(row_acc[...].astype(F32)), axis=0, keepdims=True).astype(I32)
     for c_o, k_o in others(n_c, 2):

time: 75.8 us -> 76.8 us (1.013)
  Pallas kernels: 75 us -> 76.1 us
    pallas_call x1, Pallas kernels: 74.4 us -> 75.4 us  [local_fn(): pl.pallas_call(functools.partial(kernel, dims), out_shape=(jax.ShapeDtype...]
where the time goes in v8:
time: 76.8 us; the launch traced here: 76.7 us
  Pallas kernels  76.1 us (99%)
    pallas_call x1, Pallas kernels, local_fn(): pl.pallas_call(functools.partial(kernel, dims), out_shape=(jax.ShapeDtype...  75.4 us

profile of v8, /device:TPU:1, one launch (start us, length us, event | category | flops | bytes accessed | tf_op | source)
XLA Modules:
  0.0 76.7 jit_solution(9910652567894966409)
XLA Ops:
  0.6 75.4 %shard_map.67 = (bf16[16,64]{1,0:T(8,128)(2,1)S(1)}, bf16[16,2048]{1,0:T(8,128)(2,1)S(1)}, f32[32,128]{1,0:T(8,128)S(1)}) custom-call(s32[256,16384]{1,0:T(8,128)} %mask_hbm.1, bf16[16,64]{1,0:T(8,128)(2,1)} %bitcast.8, bf16[16,2048]{1,0:T(8,128)(2,1)} %bitcast.6, s32[3,4096]{1,0:T(4,128)} %bitcast.7), custom_call_target="tpu_custom_call" | custom-call | tf_op jit(solution)/shard_map/pallas_call | solution.py:509
  76.1 0.6 shard_map.68
